TPU v7x, 32 devices: a 4x4x1 block of a 4x4x8 slice. The times are simulated.
32 devices in a mesh: dp: 1 (over z), ep: 32 (over y, x, core).
Axes of the slice: x: 4, y: 4, z: 1, core: 2. Of those that a mesh axis runs over, the one named last changes fastest.
The devices are a block of a 4x4x8 slice.
Arguments:
- x_tokens: bfloat16 [8192, 512], P(('dp', 'ep'))
- expert_ids: int32 [8192, 8], P(('dp', 'ep'))
- grad_y: bfloat16 [8192, 512], P(('dp', 'ep'))
- w_q: bfloat16 [512, 512], P('ep')
- w_k: bfloat16 [512, 512], P('ep')
- w_v: bfloat16 [512, 512], P('ep')
- w_o: bfloat16 [512, 512], P('ep')
- w_router: float32 [512, 64], replicated
- w_gate: bfloat16 [64, 512, 256], P('ep')
- w_up: bfloat16 [64, 512, 256], P('ep')
- w_down: bfloat16 [64, 256, 512], P('ep')
Outputs:
- output 1: bfloat16 [8192, 512], P(('dp', 'ep'))
- output 2: bfloat16 [8192, 512], P(('dp', 'ep'))
- output 3: bfloat16 [64, 512, 256], P(('dp', 'ep'))
- output 4: bfloat16 [64, 512, 256], P(('dp', 'ep'))
- output 5: bfloat16 [64, 256, 512], P(('dp', 'ep'))
All inputs are finite; a program needn't handle non-finite values.
Results may differ from a plain program's by a relative error of at most 0.0199931.
Values are sent between devices in bfloat16 or wider.
A program may use at most 768 MiB of HBM per device.

v0:
```python
import jax
import jax.numpy as jnp
from jax import lax
from jax.sharding import PartitionSpec as P

NORM_EPS = 1e-6
SEQ_LEN = 256
HEAD_DIM = 64


def rms_norm(values):
    wide_vals = values.astype(jnp.float32)
    return wide_vals * lax.rsqrt(jnp.mean(wide_vals * wide_vals, axis=-1, keepdims=True) + NORM_EPS)


def local_attention(q_heads, k_heads, v_heads):
    scores = jnp.einsum('bqhd,bkhd->bhqk', q_heads, k_heads, preferred_element_type=jnp.float32) * HEAD_DIM ** -0.5
    causal = jnp.arange(SEQ_LEN)[:, None] >= jnp.arange(SEQ_LEN)[None, :]
    attn_probs = jax.nn.softmax(jnp.where(causal, scores, -1e30), axis=-1).astype(jnp.bfloat16)
    return jnp.einsum('bhqk,bkhd->bqhd', attn_probs, v_heads, preferred_element_type=jnp.float32).astype(jnp.bfloat16)


def route_slots(expert_ids, experts, capacity):
    tok_count, choices = expert_ids.shape
    flat_e = expert_ids.reshape(-1)
    sort_order = jnp.argsort(flat_e, stable=True)
    counts = jnp.bincount(flat_e, length=experts)
    starts = jnp.cumsum(counts) - counts
    slot_rank = jnp.arange(capacity)
    slot_valid = (slot_rank[None, :] < counts[:, None]).reshape(-1)
    source = sort_order[jnp.minimum(starts[:, None] + slot_rank[None, :], tok_count * choices - 1)].reshape(-1)
    inverse = jnp.argsort(sort_order)
    slot_of = (flat_e * capacity + inverse - starts[flat_e]).reshape(tok_count, choices)
    return slot_of, source, slot_valid


def solution(mesh):
    group_size = mesh.shape['ep']
    tok_spec = P(('dp', 'ep'), None)
    fsdp_spec = P('ep', None)
    expert_spec = P('ep', None, None)
    grad_spec = P(('dp', 'ep'), None, None)

    def exchange(send_rows):
        return lax.all_to_all(send_rows.reshape(group_size, -1, send_rows.shape[-1]), 'ep', 0, 0, tiled=True)

    def device_step(x_tokens, expert_ids, grad_y, w_q, w_k, w_v, w_o, w_router, w_gate, w_up, w_down):
        tok_count, d_model = x_tokens.shape
        choices = expert_ids.shape[1]
        experts = w_router.shape[1]
        local_experts = w_gate.shape[0]
        avg_load = tok_count * choices // experts
        capacity = avg_load + avg_load // 2
        n_seq = tok_count // SEQ_LEN
        full_q = lax.all_gather(w_q, 'ep', axis=0, tiled=True)
        full_k = lax.all_gather(w_k, 'ep', axis=0, tiled=True)
        full_v = lax.all_gather(w_v, 'ep', axis=0, tiled=True)
        full_o = lax.all_gather(w_o, 'ep', axis=0, tiled=True)

        x_wide = x_tokens.astype(jnp.float32)
        x_norm, x_pullback = jax.vjp(rms_norm, x_wide)
        x_norm_b = x_norm.astype(jnp.bfloat16)

        def project(weight):
            heads_flat = jnp.dot(x_norm_b, weight, preferred_element_type=jnp.float32).astype(jnp.bfloat16)
            return heads_flat.reshape(n_seq, SEQ_LEN, -1, HEAD_DIM)

        attn_heads, attn_pullback = jax.vjp(local_attention, project(full_q), project(full_k), project(full_v))
        attn_proj = jnp.dot(attn_heads.reshape(tok_count, -1), full_o, preferred_element_type=jnp.float32)
        hidden = (x_wide + attn_proj).astype(jnp.bfloat16)
        h_norm, norm_pullback = jax.vjp(rms_norm, hidden.astype(jnp.float32))
        u_norm = h_norm.astype(jnp.bfloat16)
        logits = jnp.dot(h_norm, w_router, precision=lax.Precision.HIGHEST)
        gate_probs = jax.nn.softmax(jnp.take_along_axis(logits, expert_ids, axis=1), axis=-1)

        slot_of, source, slot_valid = route_slots(expert_ids, experts, capacity)
        src_token = source // choices
        send_u = jnp.where(slot_valid[:, None], u_norm[src_token], 0)
        recv_u = exchange(send_u).reshape(group_size, local_experts, capacity, d_model)
        a_gate = jnp.einsum('secd,edf->secf', recv_u, w_gate, preferred_element_type=jnp.float32)
        a_up = jnp.einsum('secd,edf->secf', recv_u, w_up, preferred_element_type=jnp.float32)
        mid_act = (jax.nn.silu(a_gate) * a_up).astype(jnp.bfloat16)
        expert_y = jnp.einsum('secf,efd->secd', mid_act, w_down, preferred_element_type=jnp.float32).astype(jnp.bfloat16)
        back_y = exchange(expert_y).reshape(-1, d_model)
        picked = back_y[slot_of].astype(jnp.float32)
        y_tokens = (hidden.astype(jnp.float32) + jnp.sum(gate_probs[:, :, None] * picked, axis=1)).astype(jnp.bfloat16)

        dy_wide = grad_y.astype(jnp.float32)
        grad_probs = jnp.sum(picked * dy_wide[:, None, :], axis=-1)
        grad_chosen = gate_probs * (grad_probs - jnp.sum(gate_probs * grad_probs, axis=-1, keepdims=True))
        grad_logits = jnp.zeros((tok_count, experts), jnp.float32).at[jnp.arange(tok_count)[:, None], expert_ids].set(grad_chosen)
        grad_hnorm = jnp.dot(grad_logits, w_router.T, precision=lax.Precision.HIGHEST)
        slot_gate = gate_probs.reshape(-1)[source]
        send_dy = jnp.where(slot_valid[:, None], slot_gate[:, None] * dy_wide[src_token], 0.0).astype(jnp.bfloat16)
        recv_dy = exchange(send_dy).reshape(group_size, local_experts, capacity, d_model)
        grad_down = jnp.einsum('secf,secd->efd', mid_act, recv_dy, preferred_element_type=jnp.float32).astype(jnp.bfloat16)
        grad_mid = jnp.einsum('secd,efd->secf', recv_dy, w_down, preferred_element_type=jnp.float32)
        sig_gate = jax.nn.sigmoid(a_gate)
        grad_agate = (grad_mid * a_up * sig_gate * (1.0 + a_gate * (1.0 - sig_gate))).astype(jnp.bfloat16)
        grad_aup = (grad_mid * a_gate * sig_gate).astype(jnp.bfloat16)
        grad_gate = jnp.einsum('secd,secf->edf', recv_u, grad_agate, preferred_element_type=jnp.float32).astype(jnp.bfloat16)
        grad_up = jnp.einsum('secd,secf->edf', recv_u, grad_aup, preferred_element_type=jnp.float32).astype(jnp.bfloat16)
        grad_recv = (jnp.einsum('secf,edf->secd', grad_agate, w_gate, preferred_element_type=jnp.float32)
                     + jnp.einsum('secf,edf->secd', grad_aup, w_up, preferred_element_type=jnp.float32)).astype(jnp.bfloat16)
        back_u = exchange(grad_recv).reshape(-1, d_model)
        grad_u = jnp.sum(back_u[slot_of].astype(jnp.float32), axis=1)
        grad_hid_b = (dy_wide + norm_pullback(grad_u + grad_hnorm)[0]).astype(jnp.bfloat16)
        grad_attn = jnp.einsum('td,hd->th', grad_hid_b, full_o, preferred_element_type=jnp.float32).astype(jnp.bfloat16)
        grad_q, grad_k, grad_v = attn_pullback(grad_attn.reshape(n_seq, SEQ_LEN, -1, HEAD_DIM))
        grad_xnorm = (jnp.einsum('th,dh->td', grad_q.reshape(tok_count, -1), full_q, preferred_element_type=jnp.float32)
                      + jnp.einsum('th,dh->td', grad_k.reshape(tok_count, -1), full_k, preferred_element_type=jnp.float32)
                      + jnp.einsum('th,dh->td', grad_v.reshape(tok_count, -1), full_v, preferred_element_type=jnp.float32))
        grad_x = (grad_hid_b.astype(jnp.float32) + x_pullback(grad_xnorm)[0]).astype(jnp.bfloat16)
        return y_tokens, grad_x, grad_gate, grad_up, grad_down

    return jax.shard_map(
        device_step, mesh=mesh,
        in_specs=(tok_spec, tok_spec, tok_spec, fsdp_spec, fsdp_spec, fsdp_spec, fsdp_spec,
                  P(None, None), expert_spec, expert_spec, expert_spec),
        out_specs=(tok_spec, tok_spec, grad_spec, grad_spec, grad_spec),
        check_vma=False)
```

profile of v0, /device:TPU:97, one launch (start us, length us, event | category | flops | bytes accessed | tf_op | source)
XLA Modules:
  0.0 474.1 jit_solution(7314083207925913873)
XLA Ops:
  3.5 32.7 %all_gather.13 = bf16[512,512]{1,0:T(8,128)(2,1)S(1)} all-gather(bf16[16,512]{1,0:T(8,128)(2,1)} %param.14), channel_id=1, replica_groups=mesh['dp'=1,'ep'=32] {'ep'}, dimensions={0}, use_global_device_ids=true | all-gather | bytes 540672 | tf_op jit(solution)/shard_map/all_gather | solution.py:55
  37.7 33.2 %all_gather.14 = bf16[512,512]{1,0:T(8,128)(2,1)S(1)} all-gather(bf16[16,512]{1,0:T(8,128)(2,1)} %param.15), channel_id=1, replica_groups=mesh['dp'=1,'ep'=32] {'ep'}, dimensions={0}, use_global_device_ids=true | all-gather | bytes 540672 | tf_op jit(solution)/shard_map/all_gather | solution.py:56
  71.4 33.2 %all_gather.12 = bf16[512,512]{1,0:T(8,128)(2,1)S(1)} all-gather(bf16[16,512]{1,0:T(8,128)(2,1)S(1)} %copy-done.42), channel_id=1, replica_groups=mesh['dp'=1,'ep'=32] {'ep'}, dimensions={0}, use_global_device_ids=true | all-gather | bytes 540672 | tf_op jit(solution)/shard_map/all_gather | solution.py:57
  106.6 33.3 %all_gather.15 = bf16[512,512]{1,0:T(8,128)(2,1)S(1)} all-gather(bf16[16,512]{1,0:T(8,128)(2,1)S(1)} %copy-done.43), channel_id=1, replica_groups=mesh['dp'=1,'ep'=32] {'ep'}, dimensions={0}, use_global_device_ids=true | all-gather | bytes 540672 | tf_op jit(solution)/shard_map/all_gather | solution.py:58
  144.7 14.7 %scatter_custom_fusion = s32[64]{0:T(128)S(1)} fusion(s32[2048]{0:T(1024)S(1)} %bitcast.256, s32[2048]{0:T(1024)S(1)} %broadcast.452, s32[]{:T(128)} %constant.31.clone.1), kind=kCustom, calls=%fused_computation.213 | custom fusion | flops 2048 | bytes 260 | tf_op jit(solution)/shard_map/scatter-add | solution.py:27
  160.0 5.0 %sort.34 = (s32[2048]{0:T(1024)}, s32[2048]{0:T(1024)S(1)}) sort(s32[2048]{0:T(1024)S(1)} %reshape.496, s32[2048]{0:T(1024)S(1)} %iota.25), dimensions={0}, to_apply=%region_7.8 | sort | flops 22528 | bytes 32768 | tf_op jit(solution)/shard_map/jit(argsort)/sort | solution.py:26
  165.1 17.4 %gather_fusion = s32[3072]{0:T(1024)S(1)} fusion(s32[2048]{0:T(1024)S(1)} %get-tuple-element.7, s32[3072]{0:T(1024)S(1)} %broadcast_clamp_fusion.2), kind=kCustom, calls=%fused_computation | custom fusion | bytes 36864 | tf_op jit(solution)/shard_map/gather | solution.py:31
  183.0 13.2 %gather_fusion.1 = bf16[3072,512]{1,0:T(8,128)(2,1)} fusion(bf16[256,512]{1,0:T(8,128)(2,1)S(1)} %multiply_convert_fusion, s32[3072]{0:T(1024)S(1)} %broadcast_clamp_fusion), kind=kCustom, calls=%fused_computation.1 | custom fusion | bytes 6303744 | tf_op jit(solution)/shard_map/gather | solution.py:78
  196.2 3.3 broadcast_select_fusion
  199.5 10.0 %all-to-all-start = ((bf16[32,96,512]{2,1,0:T(8,128)(2,1)}), bf16[32,96,512]{2,1,0:T(8,128)(2,1)}, u32[]{:S(2)}, u32[]{:S(2)}) async-start(bf16[32,96,512]{2,1,0:T(8,128)(2,1)} %broadcast_select_fusion), calls=%async_computation | async-start | bytes 6291456 | tf_op jit(solution)/shard_map/all_to_all | solution.py:45
  210.5 16.8 %gather_fusion.6 = f32[2048]{0:T(1024)S(1)} fusion(f32[256,64]{0,1:T(8,128)S(1)} %fusion.70, s32[2048]{0:T(1024)S(1)} %reshape.635), kind=kCustom, calls=%fused_computation.6 | custom fusion | bytes 32768 | tf_op jit(solution)/shard_map/jit(take_along_axis)/gather | solution.py:74
  227.8 17.4 %gather_fusion.3 = f32[3072]{0:T(1024)S(1)} fusion(f32[2048]{0:T(1024)S(1)} %div.90, s32[3072]{0:T(1024)S(1)} %broadcast_clamp_fusion.1), kind=kCustom, calls=%fused_computation.3 | custom fusion | bytes 36864 | tf_op jit(solution)/shard_map/gather | solution.py:93
  246.9 13.8 %gather_fusion.4 = f32[3072,512]{1,0:T(8,128)} fusion(f32[256,512]{1,0:T(8,128)S(1)} %convert_element_type.151, s32[3072]{0:T(1024)} %copy-done.29), kind=kCustom, calls=%fused_computation.4 | custom fusion | bytes 12595200 | tf_op jit(solution)/shard_map/gather | solution.py:94
  260.7 4.5 select_convert_fusion
  265.2 7.4 %all-to-all-start.2 = ((bf16[32,96,512]{2,1,0:T(8,128)(2,1)}), bf16[32,96,512]{2,1,0:T(8,128)(2,1)}, u32[]{:S(2)}, u32[]{:S(2)}) async-start(bf16[32,96,512]{2,1,0:T(8,128)(2,1)} %select_convert_fusion), calls=%async_computation.2 | async-start | bytes 6291456 | tf_op jit(solution)/shard_map/all_to_all | solution.py:45
  272.6 4.7 fusion.18
  277.2 4.6 fusion.20
  281.8 29.7 %all-to-all-done.2 = bf16[32,96,512]{2,1,0:T(8,128)(2,1)} async-done(((bf16[32,96,512]{2,1,0:T(8,128)(2,1)}), bf16[32,96,512]{2,1,0:T(8,128)(2,1)}, u32[]{:S(2)}, u32[]{:S(2)}) %all-to-all-start.2) | async-done | bytes 3145760 | tf_op jit(solution)/shard_map/all_to_all | solution.py:45
  311.5 7.0 %fusion.8 = (bf16[32,2,48,256]{3,2,0,1:T(8,128)(2,1)}, bf16[32,2,48,256]{3,2,0,1:T(8,128)(2,1)}, bf16[32,2,48,256]{3,2,0,1:T(8,128)(2,1)S(1)}) fusion(f32[2,32,48,256]{3,2,1,0:T(8,128)} %fusion.20, f32[2,32,48,256]{3,2,1,0:T(8,128)} %fusion.18, bf16[2,256,512]{2,1,0:T(8,128)(2,1)S(1)} %copy-done, bf16[32,2,48,512]{3,2,1,0:T(8,128)(2,1)} %bitcast.92), kind=kOutput, calls=%fused_computation.24 | convolution fusion | flops 817889280 | bytes 14680064 | tf_op jit(solution)/shard_map/secd,efd->secf/dot_general | solution.py:97
  321.4 8.7 %all-to-all-start.1 = ((bf16[32,96,512]{2,1,0:T(8,128)(2,1)}), bf16[32,96,512]{2,1,0:T(8,128)(2,1)}, u32[]{:S(2)}, u32[]{:S(2)}) async-start(bf16[32,96,512]{2,1,0:T(8,128)(2,1)} %bitcast.237), calls=%async_computation.1 | async-start | bytes 6291456 | tf_op jit(solution)/shard_map/all_to_all | solution.py:45
  330.7 5.7 %sort.35 = (s32[2048]{0:T(1024)}, s32[2048]{0:T(1024)}) sort(s32[2048]{0:T(1024)S(1)} %get-tuple-element.7, s32[2048]{0:T(1024)} %iota.26), dimensions={0}, to_apply=%region_9.10 | sort | flops 22528 | bytes 32768 | tf_op jit(solution)/shard_map/jit(argsort)/sort | solution.py:32
  339.3 5.2 %compare_select_fusion.3 = (s32[2048,1]{0,1:T(1,128)S(1)}, s32[2048,1]{0,1:T(1,128)S(1)}) fusion(s32[]{:T(128)} %bitcast.81, s32[]{:T(128)} %bitcast.82, s32[]{:T(128)} %bitcast.83, s32[]{:T(128)} %bitcast.84, s32[]{:T(128)} %bitcast.85, s32[]{:T(128)} %bitcast.87, s32[]{:T(128)} %bitcast.86, s32[2048,1]{0,1:T(1,128)} %copy-done.31), kind=kLoop, calls=%fused_computation.176 | loop fusion | flops 30720 | bytes 24604 | tf_op jit(solution)/shard_map/gather | solution.py:33
  345.9 36.8 %select_subtract_fusion = s32[2048]{0:T(1024)} fusion(pred[2048]{0:T(1024)(128)(4,1)S(1)} %get-tuple-element.67, pred[2048]{0:T(1024)(128)(4,1)S(1)} %get-tuple-element.66, pred[2048]{0:T(1024)(128)(4,1)S(1)} %get-tuple-element.65, pred[2048]{0:T(1024)(128)(4,1)S(1)} %get-tuple-element.64, pred[2048]{0:T(1024)(128)(4,1)S(1)} %get-tuple-element.63, ...), kind=kLoop, calls=%fused_computation.192 | loop fusion | flops 122880 | bytes 149732 | tf_op jit(solution)/shard_map/sub | solution.py:33
  393.5 7.4 %all-to-all-start.3 = ((bf16[32,96,512]{2,1,0:T(8,128)(2,1)}), bf16[32,96,512]{2,1,0:T(8,128)(2,1)}, u32[]{:S(2)}, u32[]{:S(2)}) async-start(bf16[32,96,512]{2,1,0:T(8,128)(2,1)} %bitcast.238), calls=%async_computation.3 | async-start | bytes 6291456 | tf_op jit(solution)/shard_map/all_to_all | solution.py:45
  409.6 4.3 fusion.42
  413.9 4.1 fusion.45
  418.1 4.0 fusion.48
  422.1 11.5 %gather_fusion.2 = bf16[2048,512]{1,0:T(8,128)(2,1)} fusion(bf16[3072,512]{1,0:T(8,128)(2,1)} %bitcast.23, s32[2048]{0:T(1024)S(1)} %broadcast_clamp_fusion.3), kind=kCustom, calls=%fused_computation.2 | custom fusion | bytes 4202496 | tf_op jit(solution)/shard_map/gather | solution.py:85
  433.6 4.2 fusion.2
  440.5 8.5 %scatter_custom_fusion.1 = f32[16384]{0:T(1024)S(1)} fusion(s32[2048]{0:T(1024)} %reshape.649, f32[2048]{0:T(1024)S(1)} %reshape.651, f32[]{:T(128)} %constant.25.clone.1), kind=kCustom, calls=%fused_computation.117 | custom fusion | bytes 66048
  449.1 11.6 %gather_fusion.5 = bf16[2048,512]{1,0:T(8,128)(2,1)} fusion(bf16[3072,512]{1,0:T(8,128)(2,1)} %bitcast.99, s32[2048]{0:T(1024)S(1)} %broadcast_clamp_fusion.3), kind=kCustom, calls=%fused_computation.5 | custom fusion | bytes 4202496 | tf_op jit(solution)/shard_map/gather | solution.py:106
  460.6 3.1 convert_reduce_fusion
  (197 shorter events, 55.1 us)
Async XLA Ops:
  0.6 310.8 %copy-start = (bf16[2,256,512]{2,1,0:T(8,128)(2,1)S(1)}, bf16[2,256,512]{2,1,0:T(8,128)(2,1)}, u32[]{:S(2)}) copy-start(bf16[2,256,512]{2,1,0:T(8,128)(2,1)} %param.21) | copy-start | bytes 1572868
  0.6 70.2 %copy-start.1 = (bf16[256,512]{1,0:T(8,128)(2,1)S(1)}, bf16[256,512]{1,0:T(8,128)(2,1)}, u32[]{:S(2)}) copy-start(bf16[256,512]{1,0:T(8,128)(2,1)} %param.11) | copy-start | bytes 786436
  0.7 70.7 %copy-start.42 = (bf16[16,512]{1,0:T(8,128)(2,1)S(1)}, bf16[16,512]{1,0:T(8,128)(2,1)}, u32[]{:S(2)}) copy-start(bf16[16,512]{1,0:T(8,128)(2,1)} %param.16) | copy-start | bytes 49156
  0.7 139.2 %copy-start.32 = (pred[256,256]{0,1:T(8,128)(4,1)}, pred[256,256]{0,1:T(8,128)(4,1)S(1)}, u32[]{:S(2)}) copy-start(pred[256,256]{0,1:T(8,128)(4,1)S(1)} %iota_compare_fusion) | copy-start | bytes 196612
  1.7 143.0 %copy-start.31 = (s32[2048,1]{0,1:T(1,128)}, s32[2048,1]{0,1:T(1,128)S(1)}, u32[]{:S(2)}) copy-start(s32[2048,1]{0,1:T(1,128)S(1)} %reshape.495) | copy-start | bytes 24580
  1.8 158.2 %copy-start.30 = (s32[2048]{0:T(1024)}, s32[2048]{0:T(1024)S(1)}, u32[]{:S(2)}) copy-start(s32[2048]{0:T(1024)S(1)} %reshape.496) | copy-start | bytes 24580
  3.5 103.1 %copy-start.38 = (f32[256]{0:T(256)}, f32[256]{0:T(256)S(1)}, u32[]{:S(2)}) copy-start(f32[256]{0:T(256)S(1)} %fusion.80) | copy-start | bytes 3076
  3.5 103.1 %copy-start.43 = (bf16[16,512]{1,0:T(8,128)(2,1)S(1)}, bf16[16,512]{1,0:T(8,128)(2,1)}, u32[]{:S(2)}) copy-start(bf16[16,512]{1,0:T(8,128)(2,1)} %param.17) | copy-start | bytes 49156
  37.7 104.4 %copy-start.24 = (bf16[256,512]{0,1:T(8,128)(2,1)}, bf16[256,512]{0,1:T(8,128)(2,1)S(1)}, u32[]{:S(2)}) copy-start(bf16[256,512]{0,1:T(8,128)(2,1)S(1)} %copy.136) | copy-start | bytes 786436
  70.9 71.2 %copy-start.3 = (bf16[512,512]{1,0:T(8,128)(2,1)}, bf16[512,512]{1,0:T(8,128)(2,1)S(1)}, u32[]{:S(2)}) copy-start(bf16[512,512]{1,0:T(8,128)(2,1)S(1)} %all_gather.14) | copy-start | bytes 1572868
  71.4 70.7 %copy-start.26 = (bf16[256,512]{0,1:T(8,128)(2,1)}, bf16[256,512]{0,1:T(8,128)(2,1)S(1)}, u32[]{:S(2)}) copy-start(bf16[256,512]{0,1:T(8,128)(2,1)S(1)} %copy.137) | copy-start | bytes 786436
  139.9 4.3 copy-start.7
  144.7 15.0 %copy-start.46 = (f32[256]{0:T(256)}, f32[256]{0:T(256)S(1)}, u32[]{:S(2)}) copy-start(f32[256]{0:T(256)S(1)} %get-tuple-element.143) | copy-start | bytes 3076
  144.7 65.1 %copy-start.40 = (f32[256]{0:T(256)}, f32[256]{0:T(256)S(1)}, u32[]{:S(2)}) copy-start(f32[256]{0:T(256)S(1)} %fusion.81) | copy-start | bytes 3076
  182.6 13.6 %copy-start.29 = (s32[3072]{0:T(1024)}, s32[3072]{0:T(1024)S(1)}, u32[]{:S(2)}) copy-start(s32[3072]{0:T(1024)S(1)} %broadcast_clamp_fusion) | copy-start | bytes 36868
  199.5 10.0 %copy-start.23 = (s32[256,8]{0,1:T(8,128)S(1)}, s32[256,8]{0,1:T(8,128)}, u32[]{:S(2)}) copy-start(s32[256,8]{0,1:T(8,128)} %param.12) | copy-start | bytes 24580
  199.5 10.3 %copy-start.21 = (f32[512,64]{0,1:T(8,128)S(1)}, f32[512,64]{0,1:T(8,128)}, u32[]{:S(2)}) copy-start(f32[512,64]{0,1:T(8,128)} %param.18) | copy-start | bytes 393220
  199.5 65.7 %all-to-all-start = ((bf16[32,96,512]{2,1,0:T(8,128)(2,1)}), bf16[32,96,512]{2,1,0:T(8,128)(2,1)}, u32[]{:S(2)}, u32[]{:S(2)}) async-start(bf16[32,96,512]{2,1,0:T(8,128)(2,1)} %broadcast_select_fusion), calls=%async_computation | async-start | bytes 6291456 | tf_op jit(solution)/shard_map/all_to_all | solution.py:45
  227.5 17.7 %copy-start.28 = (f32[256,8]{0,1:T(8,128)}, f32[256,8]{0,1:T(8,128)S(1)}, u32[]{:S(2)}) copy-start(f32[256,8]{0,1:T(8,128)S(1)} %fusion.77) | copy-start | bytes 24580
  265.2 46.3 %all-to-all-start.2 = ((bf16[32,96,512]{2,1,0:T(8,128)(2,1)}), bf16[32,96,512]{2,1,0:T(8,128)(2,1)}, u32[]{:S(2)}, u32[]{:S(2)}) async-start(bf16[32,96,512]{2,1,0:T(8,128)(2,1)} %select_convert_fusion), calls=%async_computation.2 | async-start | bytes 6291456 | tf_op jit(solution)/shard_map/all_to_all | solution.py:45
  272.6 4.7 copy-start.13
  321.4 65.7 %copy-start.48 = (s32[2]{0:T(128)S(1)}, s32[2]{0:T(128)}, u32[]{:S(2)}) copy-start(s32[2]{0:T(128)} %constant.98) | copy-start | bytes 28
  321.4 72.0 %all-to-all-start.1 = ((bf16[32,96,512]{2,1,0:T(8,128)(2,1)}), bf16[32,96,512]{2,1,0:T(8,128)(2,1)}, u32[]{:S(2)}, u32[]{:S(2)}) async-start(bf16[32,96,512]{2,1,0:T(8,128)(2,1)} %bitcast.237), calls=%async_computation.1 | async-start | bytes 6291456 | tf_op jit(solution)/shard_map/all_to_all | solution.py:45
  393.5 14.9 %copy-start.35 = (f32[8,256]{1,0:T(8,128)S(1)}, f32[8,256]{1,0:T(8,128)}, u32[]{:S(2)}) copy-start(f32[8,256]{1,0:T(8,128)} %copy-done.34) | copy-start | bytes 24580
  393.5 55.6 %all-to-all-start.3 = ((bf16[32,96,512]{2,1,0:T(8,128)(2,1)}), bf16[32,96,512]{2,1,0:T(8,128)(2,1)}, u32[]{:S(2)}, u32[]{:S(2)}) async-start(bf16[32,96,512]{2,1,0:T(8,128)(2,1)} %bitcast.238), calls=%async_computation.3 | async-start | bytes 6291456 | tf_op jit(solution)/shard_map/all_to_all | solution.py:45
  409.6 4.3 copy-start.19
  413.9 4.1 copy-start.16
  449.0 14.7 %copy-start.22 = (f32[512,64]{0,1:T(8,128)S(1)}, f32[512,64]{0,1:T(8,128)}, u32[]{:S(2)}) copy-start(f32[512,64]{0,1:T(8,128)} %param.18) | copy-start | bytes 393220
  460.6 3.9 copy-start.15
  460.6 3.9 copy-start.20
  460.6 3.9 copy-start.41
  460.6 5.6 %copy-start.8 = (bf16[512,512]{1,0:T(8,128)(2,1)S(1)}, bf16[512,512]{1,0:T(8,128)(2,1)}, u32[]{:S(2)}) copy-start(bf16[512,512]{1,0:T(8,128)(2,1)} %copy-done.7) | copy-start | bytes 1572868
  (21 other events, 43.2 us)
where the time goes:
time: 484 us; the launch traced here: 474 us
  local copies, waits for them, and re-layouts  135 us (28%)
  blocking collectives  132 us (27%)
  other arithmetic  96.5 us (20%)
  matrix products  45.2 us (9%)
  starting transfers between devices  33.4 us (7%)
  waiting for transfers between devices  29.7 us (6%)
    sub x1, other arithmetic, route_slots(): flat_e * capacity + inverse - starts[flat_e]  36.8 us
    all_to_all x4, starting transfers between devices, exchange(): lax.all_to_all(send_rows.reshape(group_size, -1, send_rows.shape[-1]), 'e...  33.4 us
    all_gather x1, blocking collectives, device_step(): full_o = lax.all_gather(w_o, 'ep', axis=0, tiled=True)  33.3 us
    all_gather x1, blocking collectives, device_step(): full_k = lax.all_gather(w_k, 'ep', axis=0, tiled=True)  33.2 us
    all_gather x1, blocking collectives, device_step(): full_v = lax.all_gather(w_v, 'ep', axis=0, tiled=True)  33.2 us
    all_gather x1, blocking collectives, device_step(): full_q = lax.all_gather(w_q, 'ep', axis=0, tiled=True)  32.7 us
    all_to_all x4, waiting for transfers between devices, exchange(): lax.all_to_all(send_rows.reshape(group_size, -1, send_rows.shape[-1]), 'e...  29.7 us
    gather x1, local copies, waits for them, and re-layouts, device_step(): slot_gate = gate_probs.reshape(-1)[source]  17.4 us
  transfers between devices with their start and end apart: 4, of which 1 were waited for; matrix products, arithmetic and copies ran while one was open for 37% of the time, Pallas kernels for 0%

commit v1 on v0

v1 whole, which is shorter than its diff:
```python
import functools
import math

import jax
import jax.numpy as jnp
from jax import lax
from jax.experimental import pallas as pl
from jax.experimental.pallas import tpu as pltpu
from jax.sharding import PartitionSpec as P

NORM_EPS = 1e-6
SEQ_LEN = 256
HEAD_DIM = 64
AXIS = 'ep'
F32 = jnp.float32
BF16 = jnp.bfloat16


class Place:
    def __init__(self, group):
        self.group = group
        self.side = math.isqrt(group // 2)
        self.me = lax.axis_index(AXIS)
        self.core = lax.rem(self.me, 2)
        self.x = lax.rem(self.me // 2, self.side)
        self.y = self.me // (2 * self.side)

    def wrap(self, v):
        return lax.rem(v + self.side, self.side)

    def at(self, dy, dx, dc=0):
        return (self.wrap(self.y + dy) * self.side + self.wrap(self.x + dx)) * 2 + lax.rem(self.core + dc, 2)


def remote(src, dst, k, target, ssem, rsem):
    return pltpu.make_async_remote_copy(src_ref=src, dst_ref=dst, send_sem=ssem.at[k], recv_sem=rsem.at[k],
                                        device_id={AXIS: target}, device_id_type=pl.DeviceIdType.MESH)


def barrier(peers):
    sem = pltpu.get_barrier_semaphore()
    for peer in peers:
        pl.semaphore_signal(sem, inc=1, device_id={AXIS: peer}, device_id_type=pl.DeviceIdType.MESH)
    pl.semaphore_wait(sem, len(peers))


def torus_peers(pl_):
    return [pl_.at(0, 1), pl_.at(0, -1), pl_.at(1, 0), pl_.at(-1, 0), pl_.at(0, 2), pl_.at(2, 0), pl_.at(0, 0, 1)]


class Sems:
    def __init__(self, ssem, rsem):
        self.ssem, self.rsem, self.used, self.sent = ssem, rsem, 0, []

    def send(self, src, dst, target):
        k = self.used
        self.used += 1
        copy = remote(src, dst, k, target, self.ssem, self.rsem)
        copy.start()
        self.sent.append(copy)
        return k

    def wait(self, k, dst, anyone):
        remote(dst, dst, k, anyone, self.ssem, self.rsem).wait_recv()


def gather_steps(place, sems, own, region, relay):
    partner = place.at(0, 0, 1)

    def dev(h, a, b, dc=0):
        return place.at(b, a, dc) if h == 0 else place.at(a, b, dc)

    def src(h, a, b, lo, num):
        return own(lo, num) if (a, b) == (0, 0) else region(dev(h, a, b), lo, num)

    def send(h, a, b, lo, num, ta, tb):
        return sems.send(src(h, a, b, lo, num), region(dev(h, a, b), lo, num), dev(h, ta, tb))

    def wait(k, h, a, b, lo, num):
        sems.wait(k, region(dev(h, a, b), lo, num), partner)

    passed = []

    def pass_on(h, a, b, lo, num):
        k = sems.send(src(h, a, b, lo, num), region(dev(h, a, b), lo, num), partner)
        passed.append((k, h, a, b, lo, num))

    halves = ((0, 0, 2), (1, 2, 2))
    first, second, rel1, rel2 = {}, {}, {}, {}
    shifts = (1, -1) if relay else (1, -1, 2)

    def go_second(h, a, lo, num):
        for s in shifts:
            second[h, a, s] = send(h, a, 0, lo, num, a, s) if False else sems.send(
                src(h, a, 0, lo, num), region(dev(h, a, 0), lo, num), dev(h, 0, s))

    for h, lo, num in halves:
        for s in shifts:
            first[h, s] = sems.send(own(lo, num), region(place.me, lo, num), dev(h, s, 0))
    for h, lo, num in halves:
        go_second(h, 0, lo, num)
    for h, lo, num in halves:
        pass_on(h, 0, 0, lo, num)
    yield
    if not relay:
        for s in shifts:
            for h, lo, num in halves:
                wait(first[h, s], h, -s, 0, lo, num)
                go_second(h, -s, lo, num)
                pass_on(h, -s, 0, lo, num)
            yield
        for a in (0, -1, 1, -2):
            for s in shifts:
                for h, lo, num in halves:
                    wait(second[h, a, s], h, a, -s, lo, num)
                    pass_on(h, a, -s, lo, num)
            yield
    else:
        for s in shifts:
            for h, lo, num in halves:
                wait(first[h, s], h, -s, 0, lo, num)
                part = lo + (s == -1)
                rel1[h, s] = sems.send(src(h, -s, 0, part, 1), region(dev(h, -s, 0), part, 1), dev(h, s, 0))
                go_second(h, -s, lo, num)
                pass_on(h, -s, 0, lo, num)
            yield

        def relay2(h, lo, num, a, s):
            wait(second[h, a, s], h, a, -s, lo, num)
            part = lo + (s == -1)
            rel2[h, a, s] = sems.send(src(h, a, -s, part, 1), region(dev(h, a, -s), part, 1), dev(h, 0, s))
            pass_on(h, a, -s, lo, num)

        for h, lo, num in halves:
            for s in shifts:
                relay2(h, lo, num, 0, s)
        yield
        for h, lo, num in halves:
            for s in shifts:
                wait(rel1[h, s], h, -2 * s, 0, lo + (s == -1), 1)
            go_second(h, 2, lo, num)
            pass_on(h, 2, 0, lo, num)
        yield
        for a in (-1, 1, 2):
            for s in shifts:
                for h, lo, num in halves:
                    relay2(h, lo, num, a, s)
            yield
        for a in (0, -1, 1, 2):
            for h, lo, num in halves:
                for s in shifts:
                    wait(rel2[h, a, s], h, a, -2 * s, lo + (s == -1), 1)
                pass_on(h, a, 2, lo, num)
            yield
    for k, h, a, b, lo, num in passed:
        yy = dev(h, a, b, 1)
        sems.wait(k, region(yy, lo, num), partner)
    yield


def run_all(gens):
    gens = list(gens)
    while gens:
        alive = []
        for g in gens:
            try:
                next(g)
                alive.append(g)
            except StopIteration:
                pass
        gens = alive


def rows_region(ref, quarter):
    return lambda d, lo, num: ref.at[d, pl.ds(lo * quarter, num * quarter)]


def rows_own(ref, quarter):
    return lambda lo, num: ref.at[pl.ds(lo * quarter, num * quarter)]


def weights_kernel(group, w_ref, dy_ref, full_ref, dy_all_ref, ssem, rsem):
    place = Place(group)
    barrier(torus_peers(place))
    sems = Sems(ssem, rsem)
    depth = w_ref.shape[1]
    mine = pl.ds(pl.multiple_of(place.me * depth, depth), depth)
    full_ref[:, mine, :] = w_ref[...]
    dy_all_ref[place.me] = dy_ref[...]
    w_steps = gather_steps(
        place, sems, lambda lo, num: w_ref.at[pl.ds(lo, num)],
        lambda d, lo, num: full_ref.at[pl.ds(lo, num), pl.ds(pl.multiple_of(d * depth, depth), depth)], False)
    quarter = dy_ref.shape[0] // 4
    dy_steps = gather_steps(place, sems, rows_own(dy_ref, quarter), rows_region(dy_all_ref, quarter), True)
    run_all([w_steps, dy_steps])
    for copy in sems.sent:
        copy.wait_send()


def tokens_kernel(group, u_ref, meta_ref, u_all_ref, meta_all_ref, ssem, rsem):
    place = Place(group)
    barrier(torus_peers(place))
    sems = Sems(ssem, rsem)
    u_all_ref[place.me] = u_ref[...]
    meta_all_ref[place.me] = meta_ref[...]
    quarter = u_ref.shape[0] // 4
    m_steps = gather_steps(place, sems, lambda lo, num: meta_ref.at[pl.ds(lo, num)],
                           lambda d, lo, num: meta_all_ref.at[d, pl.ds(lo, num)], False)
    u_steps = gather_steps(place, sems, rows_own(u_ref, quarter), rows_region(u_all_ref, quarter), True)
    run_all([m_steps, u_steps])
    for copy in sems.sent:
        copy.wait_send()


def return_kernel(group, z_ref, du_ref, z_back_ref, du_back_ref, ssem, rsem):
    place = Place(group)
    side = place.side
    offs = [(dy, dx, dc) for dy in range(side) for dx in range(side) for dc in range(2)][1:]
    barrier([place.at(*o) for o in offs])
    sems = Sems(ssem, rsem)
    waits = []
    for out, back in ((z_ref, z_back_ref), (du_ref, du_back_ref)):
        back[place.me] = out[place.me]
        for i in range(len(offs)):
            dy, dx, dc = offs[(i * 12) % len(offs)]
            target = place.at(dy, dx, dc)
            k = sems.send(out.at[target], back.at[place.me], target)
            waits.append((k, back, place.at(-dy, -dx, dc)))
    for k, back, origin in waits:
        sems.wait(k, back.at[origin], origin)
    for copy in sems.sent:
        copy.wait_send()


def comm_call(kernel, group, outs, sems, cid, name):
    vmem = pl.BlockSpec(memory_space=pltpu.VMEM)
    return lambda *args: pl.pallas_call(
        functools.partial(kernel, group), out_shape=outs,
        in_specs=[vmem] * len(args), out_specs=[vmem] * len(outs),
        scratch_shapes=[pltpu.SemaphoreType.DMA((sems,)), pltpu.SemaphoreType.DMA((sems,))],
        compiler_params=pltpu.CompilerParams(collective_id=cid, has_side_effects=True, vmem_limit_bytes=60 << 20),
        name=name)(*args)


def rms_norm(values):
    wide_vals = values.astype(F32)
    return wide_vals * lax.rsqrt(jnp.mean(wide_vals * wide_vals, axis=-1, keepdims=True) + NORM_EPS)


def local_attention(q_heads, k_heads, v_heads):
    scores = jnp.einsum('bqhd,bkhd->bhqk', q_heads, k_heads, preferred_element_type=F32) * HEAD_DIM ** -0.5
    causal = jnp.arange(SEQ_LEN)[:, None] >= jnp.arange(SEQ_LEN)[None, :]
    attn_probs = jax.nn.softmax(jnp.where(causal, scores, -1e30), axis=-1).astype(BF16)
    return jnp.einsum('bhqk,bkhd->bqhd', attn_probs, v_heads, preferred_element_type=F32).astype(BF16)


def mm(a, b, dims):
    return lax.dot_general(a, b, dims, preferred_element_type=F32)


def solution(mesh):
    group = mesh.shape[AXIS]
    tok_spec = P(('dp', 'ep'), None)
    fsdp_spec = P('ep', None)
    expert_spec = P('ep', None, None)
    grad_spec = P(('dp', 'ep'), None, None)

    def device_step(x_tokens, expert_ids, grad_y, w_q, w_k, w_v, w_o, w_router, w_gate, w_up, w_down):
        toks, d_model = x_tokens.shape
        choices = expert_ids.shape[1]
        experts = w_router.shape[1]
        local = w_gate.shape[0]
        avg_load = toks * choices // experts
        cap = avg_load + avg_load // 2
        n_seq = toks // SEQ_LEN
        shape = jax.ShapeDtypeStruct
        depth = w_q.shape[0]

        w_own = jnp.stack([w_q, w_k, w_v, w_o])
        w_full, dy_all = comm_call(
            weights_kernel, group,
            [shape((4, group * depth, d_model), BF16), shape((group, toks, d_model), BF16)], 176, 1, 'gather_w')(w_own, grad_y)
        full_q, full_k, full_v, full_o = w_full[0], w_full[1], w_full[2], w_full[3]

        x_wide = x_tokens.astype(F32)
        x_norm, x_pullback = jax.vjp(rms_norm, x_wide)
        x_norm_b = x_norm.astype(BF16)

        def project(weight):
            heads_flat = jnp.dot(x_norm_b, weight, preferred_element_type=F32).astype(BF16)
            return heads_flat.reshape(n_seq, SEQ_LEN, -1, HEAD_DIM)

        attn_heads, attn_pullback = jax.vjp(local_attention, project(full_q), project(full_k), project(full_v))
        attn_proj = jnp.dot(attn_heads.reshape(toks, -1), full_o, preferred_element_type=F32)
        hidden = (x_wide + attn_proj).astype(BF16)
        h_norm, norm_pullback = jax.vjp(rms_norm, hidden.astype(F32))
        u_norm = h_norm.astype(BF16)
        logits = jnp.dot(h_norm, w_router, precision=lax.Precision.HIGHEST)

        lane_e = jnp.arange(experts)
        hit = expert_ids[:, :, None] == lane_e
        chosen = jnp.any(hit, axis=1)
        earlier = (jnp.arange(toks)[:, None] > jnp.arange(toks)[None, :]).astype(BF16)
        rank = jnp.dot(earlier, chosen.astype(BF16), preferred_element_type=F32)
        top = jnp.max(jnp.where(chosen, logits, -jnp.inf), axis=-1, keepdims=True)
        expd = jnp.where(chosen, jnp.exp(logits - top), 0.0)
        gates = expd / jnp.sum(expd, axis=-1, keepdims=True)
        gate_j = jnp.sum(jnp.where(hit, gates[:, None, :], 0.0), axis=-1)

        meta = jnp.concatenate([expert_ids.astype(F32).T, gate_j.T], axis=0).reshape(4, 4, toks)
        u_all, meta_all = comm_call(
            tokens_kernel, group,
            [shape((group, toks, d_model), BF16), shape((group, 4, 4, toks), F32)], 176, 2, 'gather_u')(u_norm, meta)
        meta_all = meta_all.reshape(group, 2, choices, toks)

        mine = lax.axis_index(AXIS) * local + jnp.arange(local)
        hits = meta_all[:, 0][:, None] == mine.astype(F32)[None, :, None, None]
        sel = jnp.any(hits, axis=2)
        gate_here = jnp.sum(jnp.where(hits, meta_all[:, 1][:, None], 0.0), axis=2)
        later = (jnp.arange(toks)[:, None] < jnp.arange(toks)[None, :]).astype(BF16)
        rank_here = mm(sel.astype(BF16), later, (((2,), (0,)), ((), ())))
        pick = sel[:, :, None, :] & (rank_here[:, :, None, :] == jnp.arange(cap, dtype=F32)[None, None, :, None])
        slot_gate = jnp.sum(jnp.where(pick, gate_here[:, :, None, :], 0.0), axis=-1).reshape(group, local * cap)
        pick_b = pick.astype(BF16).reshape(group, local * cap, toks)
        batched = (((2,), (1,)), ((0,), (0,)))
        recv_u = mm(pick_b, u_all, batched).astype(BF16).reshape(group, local, cap, d_model)
        raw_dy = mm(pick_b, dy_all, batched)
        recv_dy = (slot_gate[:, :, None] * raw_dy).astype(BF16).reshape(group, local, cap, d_model)

        a_gate = jnp.einsum('secd,edf->secf', recv_u, w_gate, preferred_element_type=F32)
        a_up = jnp.einsum('secd,edf->secf', recv_u, w_up, preferred_element_type=F32)
        mid_act = (jax.nn.silu(a_gate) * a_up).astype(BF16)
        expert_y = jnp.einsum('secf,efd->secd', mid_act, w_down, preferred_element_type=F32).astype(BF16)
        grad_down = jnp.einsum('secf,secd->efd', mid_act, recv_dy, preferred_element_type=F32).astype(BF16)
        grad_mid = jnp.einsum('secd,efd->secf', recv_dy, w_down, preferred_element_type=F32)
        sig_gate = jax.nn.sigmoid(a_gate)
        grad_agate = (grad_mid * a_up * sig_gate * (1.0 + a_gate * (1.0 - sig_gate))).astype(BF16)
        grad_aup = (grad_mid * a_gate * sig_gate).astype(BF16)
        grad_gate = jnp.einsum('secd,secf->edf', recv_u, grad_agate, preferred_element_type=F32).astype(BF16)
        grad_up = jnp.einsum('secd,secf->edf', recv_u, grad_aup, preferred_element_type=F32).astype(BF16)
        grad_recv = (jnp.einsum('secf,edf->secd', grad_agate, w_gate, preferred_element_type=F32)
                     + jnp.einsum('secf,edf->secd', grad_aup, w_up, preferred_element_type=F32)).astype(BF16)

        rows = shape((group, local * cap, d_model), BF16)
        back_z, back_u = comm_call(return_kernel, group, [rows, rows], 2 * group, 3, 'return_rows')(
            expert_y.reshape(rows.shape), grad_recv.reshape(rows.shape))
        back_z = back_z.reshape(-1, d_model)
        back_u = back_u.reshape(-1, d_model)

        slots = experts * cap
        column = jnp.arange(slots)
        spread = (lane_e[:, None] == (column // cap)[None, :]).astype(BF16)
        rank_x = jnp.dot(jnp.where(chosen, rank, -1.0).astype(BF16), spread, preferred_element_type=F32)
        place = rank_x == (column % cap).astype(F32)[None, :]
        gate_x = jnp.dot(gates, spread.astype(F32), precision=lax.Precision.HIGHEST)
        mixed = jnp.dot(jnp.where(place, gate_x, 0.0), back_z.astype(F32), precision=lax.Precision.HIGHEST)
        y_tokens = (hidden.astype(F32) + mixed).astype(BF16)

        dy_wide = grad_y.astype(F32)
        score = mm(grad_y, back_z, (((1,), (1,)), ((), ())))
        grad_gates = jnp.dot(jnp.where(place, score, 0.0), spread.astype(F32).T, precision=lax.Precision.HIGHEST)
        grad_logits = gates * (grad_gates - jnp.sum(gates * grad_gates, axis=-1, keepdims=True))
        grad_hnorm = jnp.dot(grad_logits, w_router.T, precision=lax.Precision.HIGHEST)
        grad_u = jnp.dot(place.astype(BF16), back_u, preferred_element_type=F32)
        grad_hid_b = (dy_wide + norm_pullback(grad_u + grad_hnorm)[0]).astype(BF16)
        grad_attn = jnp.einsum('td,hd->th', grad_hid_b, full_o, preferred_element_type=F32).astype(BF16)
        grad_q, grad_k, grad_v = attn_pullback(grad_attn.reshape(n_seq, SEQ_LEN, -1, HEAD_DIM))
        grad_xnorm = (jnp.einsum('th,dh->td', grad_q.reshape(toks, -1), full_q, preferred_element_type=F32)
                      + jnp.einsum('th,dh->td', grad_k.reshape(toks, -1), full_k, preferred_element_type=F32)
                      + jnp.einsum('th,dh->td', grad_v.reshape(toks, -1), full_v, preferred_element_type=F32))
        grad_x = (grad_hid_b.astype(F32) + x_pullback(grad_xnorm)[0]).astype(BF16)
        return y_tokens, grad_x, grad_gate, grad_up, grad_down

    return jax.shard_map(
        device_step, mesh=mesh,
        in_specs=(tok_spec, tok_spec, tok_spec, fsdp_spec, fsdp_spec, fsdp_spec, fsdp_spec,
                  P(None, None), expert_spec, expert_spec, expert_spec),
        out_specs=(tok_spec, tok_spec, grad_spec, grad_spec, grad_spec),
        check_vma=False)
```

time: 484 us -> 256 us (0.53); the launches traced: 474 us -> 252 us
  Pallas kernels: 0 us -> 169 us
  blocking collectives: 132 us -> 0 us
  local copies, waits for them, and re-layouts: 135 us -> 9.54 us
  other arithmetic: 96.5 us -> 8.4 us
  starting transfers between devices: 33.4 us -> 0 us
  waiting for transfers between devices: 29.7 us -> 0 us
  matrix products: 45.2 us -> 63.4 us
    pallas_call x0 -> x3, Pallas kernels: none -> 169 us  [comm_call(): pl.pallas_call(functools.partial(kernel, group), out_shape=outs, in_specs...]
    all_gather x4 -> x0, blocking collectives: 132 us -> none  [the longest x1 33.3 us: device_step(): full_o = lax.all_gather(w_o, 'ep', axis=0, tiled=True)]
    gather x16 -> x0, local copies, waits for them, and re-layouts: 105 us -> none  [the longest x1 17.4 us: device_step(): slot_gate = gate_probs.reshape(-1)[source]]
    sub x2 -> x0, other arithmetic: 36.8 us -> none  [the longest x1 36.8 us: route_slots(): flat_e * capacity + inverse - starts[flat_e]]
    all_to_all x4 -> x0, starting transfers between devices: 33.4 us -> none  [exchange(): lax.all_to_all(send_rows.reshape(group_size, -1, send_rows.shape[-1]), 'e...]
    all_to_all x4 -> x0, waiting for transfers between devices: 29.7 us -> none  [exchange(): lax.all_to_all(send_rows.reshape(group_size, -1, send_rows.shape[-1]), 'e...]
    dot_general x19 -> x28, matrix products: 38.6 us -> 56.7 us  [the longest x4 24.1 us: mm(): return lax.dot_general(a, b, dims, preferred_element_type=F32)]
    scatter-add x1 -> x0, other arithmetic: 14.7 us -> none  [route_slots(): counts = jnp.bincount(flat_e, length=experts)]
  transfers between devices with their start and end apart: 4 -> 0, of which waited for: 1 -> 0; matrix products, arithmetic and copies ran while one was open for 37% -> 0% of each run, Pallas kernels for 0% -> 0%
where the time goes in v1:
time: 256 us; the launch traced here: 252 us
  Pallas kernels  169 us (66%)
  matrix products  63.4 us (25%)
  local copies, waits for them, and re-layouts  9.54 us (4%)
  other arithmetic  8.4 us (3%)
    pallas_call x3, Pallas kernels, comm_call(): pl.pallas_call(functools.partial(kernel, group), out_shape=outs, in_specs...  169 us
    dot_general x4, matrix products, mm(): return lax.dot_general(a, b, dims, preferred_element_type=F32)  24.1 us

profile of v1, /device:TPU:97, one launch (start us, length us, event | category | flops | bytes accessed | tf_op | source)
XLA Modules:
  0.0 252.0 jit_solution(18158377715069740386)
XLA Ops:
  0.6 1.5 pad_maximum_fusion.w_ref
  2.1 47.2 %gather_w.1 = (bf16[4,512,512]{2,1,0:T(8,128)(2,1)}, bf16[32,256,512]{2,1,0:T(8,128)(2,1)}) custom-call(bf16[4,16,512]{2,1,0:T(8,128)(2,1)} %pad_maximum_fusion.w_ref, bf16[256,512]{1,0:T(8,128)(2,1)} %dy_ref.1), custom_call_target="tpu_custom_call" | custom-call | tf_op jit(solution)/shard_map/gather_w/pallas_call | solution.py:237
  49.4 1.1 fusion.65
  50.5 1.5 convolution_convert_fusion.8
  52.1 1.6 convolution_convert_fusion.7
  53.9 2.1 fusion.129
  56.0 1.8 divide_convert_fusion
  57.8 1.4 convolution_convert_fusion.9
  59.7 1.4 multiply_reduce_fusion.1
  63.5 36.6 %gather_u.1 = (bf16[32,256,512]{2,1,0:T(8,128)(2,1)}, f32[32,4,4,256]{3,2,1,0:T(4,128)}) custom-call(bf16[256,512]{1,0:T(8,128)(2,1)} %multiply_convert_fusion.1.u_ref, f32[4,4,256]{2,1,0:T(4,128)} %reshape.211.meta_ref), custom_call_target="tpu_custom_call" | custom-call | tf_op jit(solution)/shard_map/gather_u/pallas_call | solution.py:237
  100.1 1.2 reshape.212
  103.7 16.2 %multiply_convert_fusion = bf16[32,96,512]{2,1,0:T(8,128)(2,1)S(1)} fusion(f32[32,96]{1,0:T(8,128)S(1)} %mul.159, pred[32,96,256]{2,1,0:T(32,128)(4,1)S(1)} %fusion.14, bf16[32,256,512]{2,1,0:T(8,128)(2,1)} %get-tuple-element.14), kind=kOutput, calls=%fused_computation.2 | convolution fusion | flops 808452096 | bytes 12333056 | tf_op jit(solution)/shard_map/dot_general | solution.py:258
  119.9 4.8 %convolution_convert_fusion = bf16[32,96,512]{2,1,0:T(8,128)(2,1)S(1)} fusion(pred[32,96,256]{2,1,0:T(32,128)(4,1)S(1)} %fusion.14, bf16[32,256,512]{2,1,0:T(8,128)(2,1)} %get-tuple-element.13), kind=kOutput, calls=%fused_computation.40 | convolution fusion | flops 806879232 | bytes 12320768 | tf_op jit(solution)/shard_map/dot_general | solution.py:258
  125.8 1.0 fusion.21
  126.8 2.1 fusion.7
  128.9 1.8 fusion.43
  130.7 2.2 fusion.46
  132.9 2.2 fusion.49
  135.1 1.0 fusion.70
  136.1 1.1 fusion.2
  137.2 1.9 copy.69
  139.1 1.0 convert_bitcast_fusion
  140.1 2.0 copy.67
  142.1 85.3 %return_rows.1 = (bf16[32,96,512]{2,1,0:T(8,128)(2,1)}, bf16[32,96,512]{2,1,0:T(8,128)(2,1)}) custom-call(bf16[32,96,512]{2,1,0:T(8,128)(2,1)} %bitcast.206, bf16[32,96,512]{2,1,0:T(8,128)(2,1)} %bitcast.205), custom_call_target="tpu_custom_call" | custom-call | tf_op jit(solution)/shard_map/return_rows/pallas_call | solution.py:237
  228.4 2.9 %fusion.1 = f32[256,3072]{1,0:T(8,128)S(1)} fusion(pred[256,3072]{1,0:T(32,128)(4,1)S(1)} %convolution_compare_fusion, bf16[3072,512]{1,0:T(8,128)(2,1)} %bitcast.203, bf16[256,512]{1,0:T(8,128)(2,1)S(1)} %copy-done.3), kind=kOutput, calls=%fused_computation.5 | convolution fusion | flops 806092800 | bytes 7340032 | tf_op jit(solution)/shard_map/dot_general | solution.py:258
  231.3 1.8 multiply_reduce_fusion.2
  233.2 1.2 fusion.130
  236.1 2.1 convolution_convert_fusion.5
  238.1 1.1 copy.71
  239.7 2.3 fusion.28
  246.7 1.6 convolution_select_fusion
  248.3 3.3 %fusion.52 = bf16[256,512]{1,0:T(8,128)(2,1)} fusion(f32[256,512]{1,0:T(8,128)S(1)} %get-tuple-element.25, f32[256,3072]{1,0:T(8,128)S(1)} %convolution_select_fusion, bf16[3072,512]{1,0:T(8,128)(2,1)S(1)} %bitcast.204), kind=kOutput, calls=%fused_computation.67 | convolution fusion | flops 4832100352 | bytes 7077888 | tf_op jit(solution)/shard_map/dot_general | solution.py:356
  (85 shorter events, 14.1 us)
Async XLA Ops:
  0.6 126.1 %copy-start = (bf16[2,256,512]{2,1,0:T(8,128)(2,1)S(1)}, bf16[2,256,512]{2,1,0:T(8,128)(2,1)}, u32[]{:S(2)}) copy-start(bf16[2,256,512]{2,1,0:T(8,128)(2,1)} %param.21) | copy-start | bytes 1572868
  52.1 5.7 %copy-start.13 = (bf16[256,512]{0,1:T(8,128)(2,1)}, bf16[256,512]{0,1:T(8,128)(2,1)S(1)}, u32[]{:S(2)}) copy-start(bf16[256,512]{0,1:T(8,128)(2,1)S(1)} %copy.60) | copy-start | bytes 786436
  53.8 4.0 %copy-start.15 = (bf16[256,512]{0,1:T(8,128)(2,1)}, bf16[256,512]{0,1:T(8,128)(2,1)S(1)}, u32[]{:S(2)}) copy-start(bf16[256,512]{0,1:T(8,128)(2,1)S(1)} %copy.61) | copy-start | bytes 786436
  53.8 2.2 copy-start.18
  53.8 4.0 %copy-start.4 = (bf16[256,512]{1,0:T(8,128)(2,1)S(1)}, bf16[256,512]{1,0:T(8,128)(2,1)}, u32[]{:S(2)}) copy-start(bf16[256,512]{1,0:T(8,128)(2,1)} %param.11) | copy-start | bytes 786436
  57.8 4.2 %copy-start.17 = (s32[256,8]{0,1:T(8,128)S(1)}, s32[256,8]{0,1:T(8,128)}, u32[]{:S(2)}) copy-start(s32[256,8]{0,1:T(8,128)} %param.12) | copy-start | bytes 24580
  57.8 4.2 %copy-start.11 = (f32[512,64]{0,1:T(8,128)S(1)}, f32[512,64]{0,1:T(8,128)}, u32[]{:S(2)}) copy-start(f32[512,64]{0,1:T(8,128)} %param.18) | copy-start | bytes 393220
  119.9 4.8 %copy-start.7 = (bf16[2,512,256]{2,1,0:T(8,128)(2,1)S(1)}, bf16[2,512,256]{2,1,0:T(8,128)(2,1)}, u32[]{:S(2)}) copy-start(bf16[2,512,256]{2,1,0:T(8,128)(2,1)} %param.20) | copy-start | bytes 1572868
  124.7 1.0 copy-start.6
  227.5 1.0 copy-start.3
  231.3 1.9 copy-start.20
  233.1 1.3 copy-start.12
  235.4 0.7 copy-start.9
  239.2 2.8 %copy-start.2 = (f32[8,256,256]{1,2,0:T(8,128)S(1)}, f32[8,256,256]{1,2,0:T(8,128)}, u32[]{:S(2)}) copy-start(f32[8,256,256]{1,2,0:T(8,128)} %get-tuple-element.23) | copy-start | bytes 6291460
  239.2 2.8 %copy-start.14 = (bf16[256,512]{0,1:T(8,128)(2,1)S(1)}, bf16[256,512]{0,1:T(8,128)(2,1)}, u32[]{:S(2)}) copy-start(bf16[256,512]{0,1:T(8,128)(2,1)} %copy-done.13) | copy-start | bytes 786436
  239.3 2.8 %copy-start.19 = (pred[256,256]{0,1:T(8,128)(4,1)S(1)}, pred[256,256]{0,1:T(8,128)(4,1)}, u32[]{:S(2)}) copy-start(pred[256,256]{0,1:T(8,128)(4,1)} %copy-done.18) | copy-start | bytes 196612
  242.1 1.0 copy-start.16
  243.1 1.6 copy-start.8
  243.7 1.6 copy-start.5
  243.7 2.1 copy-start.10
  245.8 2.5 %copy-start.1 = (bf16[32,96,512]{2,1,0:T(8,128)(2,1)S(1)}, bf16[32,96,512]{2,1,0:T(8,128)(2,1)}, u32[]{:S(2)}) copy-start(bf16[32,96,512]{2,1,0:T(8,128)(2,1)} %get-tuple-element.15) | copy-start | bytes 9437188

commit v2 on v1

v2 whole, which is shorter than its diff:
```python
import functools
import math

import jax
import jax.numpy as jnp
from jax import lax
from jax.experimental import pallas as pl
from jax.experimental.pallas import tpu as pltpu
from jax.sharding import PartitionSpec as P

NORM_EPS = 1e-6
SEQ_LEN = 256
HEAD_DIM = 64
AXIS = 'ep'
F32 = jnp.float32
BF16 = jnp.bfloat16


class Place:
    def __init__(self, group):
        self.group = group
        self.side = math.isqrt(group // 2)
        self.me = lax.axis_index(AXIS)
        self.core = lax.rem(self.me, 2)
        self.x = lax.rem(self.me // 2, self.side)
        self.y = self.me // (2 * self.side)

    def wrap(self, v):
        return lax.rem(v + self.side, self.side)

    def at(self, dy, dx, dc=0):
        return (self.wrap(self.y + dy) * self.side + self.wrap(self.x + dx)) * 2 + lax.rem(self.core + dc, 2)


def remote(src, dst, k, target, ssem, rsem):
    return pltpu.make_async_remote_copy(src_ref=src, dst_ref=dst, send_sem=ssem.at[k], recv_sem=rsem.at[k],
                                        device_id={AXIS: target}, device_id_type=pl.DeviceIdType.MESH)


def near_peers(pl_):
    return [pl_.at(0, 1), pl_.at(0, -1), pl_.at(1, 0), pl_.at(-1, 0), pl_.at(0, 2), pl_.at(2, 0), pl_.at(0, 0, 1)]


class Sems:
    def __init__(self, ssem, rsem):
        self.ssem, self.rsem, self.used, self.sent = ssem, rsem, 0, []

    def send(self, src, dst, target):
        k = self.used
        self.used += 1
        copy = remote(src, dst, k, target, self.ssem, self.rsem)
        copy.start()
        self.sent.append(copy)
        return k

    def wait(self, k, dst, anyone):
        remote(dst, dst, k, anyone, self.ssem, self.rsem).wait_recv()


def gather_steps(place, sems, region, pieces, relay, halves):
    partner = place.at(0, 0, 1)

    def dev(h, a, b, dc=0):
        return place.at(b, a, dc) if h == 0 else place.at(a, b, dc)

    def send(h, a, b, lo, num, target):
        where = region(dev(h, a, b), lo, num)
        return sems.send(where, where, target)

    def wait(k, h, a, b, lo, num):
        sems.wait(k, region(dev(h, a, b), lo, num), partner)

    passed = []

    def pass_on(h, a, b, lo, num):
        passed.append((send(h, a, b, lo, num, partner), h, a, b, lo, num))

    first, second, rel1, rel2 = {}, {}, {}, {}
    shifts = (1, -1) if relay else (1, -1, 2)

    def go_second(h, a, lo, num):
        for s in shifts:
            second[h, a, s] = send(h, a, 0, lo, num, dev(h, 0, s))

    for h, lo, num in halves:
        for s in shifts:
            first[h, s] = send(h, 0, 0, lo, num, dev(h, s, 0))
    for h, lo, num in halves:
        go_second(h, 0, lo, num)
    for h, lo, num in halves:
        pass_on(h, 0, 0, lo, num)
    yield
    if not relay:
        for s in shifts:
            for h, lo, num in halves:
                wait(first[h, s], h, -s, 0, lo, num)
                go_second(h, -s, lo, num)
                pass_on(h, -s, 0, lo, num)
            yield
        for a in (0, -1, 1, -2):
            for s in shifts:
                for h, lo, num in halves:
                    wait(second[h, a, s], h, a, -s, lo, num)
                    pass_on(h, a, -s, lo, num)
            yield
    else:
        for s in shifts:
            for h, lo, num in halves:
                wait(first[h, s], h, -s, 0, lo, num)
                part = lo + (s == -1)
                rel1[h, s] = send(h, -s, 0, part, 1, dev(h, s, 0))
                go_second(h, -s, lo, num)
                pass_on(h, -s, 0, lo, num)
            yield

        def relay2(h, lo, num, a, s):
            wait(second[h, a, s], h, a, -s, lo, num)
            part = lo + (s == -1)
            rel2[h, a, s] = send(h, a, -s, part, 1, dev(h, 0, s))
            pass_on(h, a, -s, lo, num)

        for h, lo, num in halves:
            for s in shifts:
                relay2(h, lo, num, 0, s)
        yield
        for h, lo, num in halves:
            for s in shifts:
                wait(rel1[h, s], h, -2 * s, 0, lo + (s == -1), 1)
            go_second(h, 2, lo, num)
            pass_on(h, 2, 0, lo, num)
        yield
        for a in (-1, 1, 2):
            for s in shifts:
                for h, lo, num in halves:
                    relay2(h, lo, num, a, s)
            yield
        for a in (0, -1, 1, 2):
            for h, lo, num in halves:
                for s in shifts:
                    wait(rel2[h, a, s], h, a, -2 * s, lo + (s == -1), 1)
                pass_on(h, a, 2, lo, num)
            yield
    for k, h, a, b, lo, num in passed:
        sems.wait(k, region(dev(h, a, b, 1), lo, num), partner)
    yield


def finish(*gens):
    gens = list(gens)
    while gens:
        gens = [g for g in gens if next(g, gens) is not gens]


NN = (((1,), (0,)), ((), ()))
NT = (((1,), (1,)), ((), ()))
TN = (((0,), (0,)), ((), ()))
EXACT = lax.Precision.HIGHEST


def mm(a, b, dims=NN, precision=None):
    return lax.dot_general(a, b, dims, precision=precision, preferred_element_type=F32)


def three(v):
    a = v.astype(BF16)
    v = v - a.astype(F32)
    b = v.astype(BF16)
    return a, b, (v - b.astype(F32)).astype(BF16)


def iota(shape, dim):
    return lax.broadcasted_iota(jnp.int32, shape, dim)


def inv_rms(v):
    return lax.rsqrt(jnp.mean(v * v, axis=-1, keepdims=True) + NORM_EPS)


def rms_back(v, inv, g):
    return inv * g - v * (inv * inv * inv * jnp.mean(g * v, axis=-1, keepdims=True))


def block_offset(i, place):
    g, b = i // (2 * place.side), lax.rem(i, 2 * place.side)
    dx, dc = b // 2, lax.rem(b, 2)
    return lax.rem(g + dx, place.side), dx, dc


def layer_kernel(group, experts, cap, x_ref, idst_ref, dy_ref, wq_ref, wk_ref, wv_ref, wo_ref, wr_ref, wg_ref, wu_ref, wd_ref,
                 y_ref, gx_ref, gg_ref, gu_ref, gd_ref,
                 w_full, u_all, dy_all, ids_all, g_all, m_s, r_s, pick_s, ru_s, rdy_s, ag_s, au_s, mid_s, dag_s, dau_s,
                 zback, dback, prob_s, q_s, k_s, v_s, o_s, hid_s, place_s,
                 lsem, ssem, rsem):
    place = Place(group)
    me = place.me
    toks, d_model = x_ref.shape
    choices = idst_ref.shape[0]
    local, _, ff = wg_ref.shape
    depth = wq_ref.shape[0]
    per = 2 * place.side
    groups = group // per
    sems = Sems(ssem, rsem)

    def rows_of(d):
        return pl.ds(pl.multiple_of(d * depth, depth), depth)

    own_w = [pltpu.make_async_copy(w, w_full.at[i, rows_of(me)], lsem.at[i]) for i, w in enumerate((wq_ref, wk_ref, wv_ref, wo_ref))]
    for copy in own_w:
        copy.start()
    sem = pltpu.get_barrier_semaphore()
    peers = near_peers(place)
    for peer in peers:
        pl.semaphore_signal(sem, inc=1, device_id={AXIS: peer}, device_id_type=pl.DeviceIdType.MESH)

    dy_all[me] = dy_ref[...]
    idst = idst_ref[...].astype(F32)
    ids_all[me] = idst
    lane_e = iota((2 * experts, toks), 0).astype(F32)
    chosen_t = jnp.zeros((2 * experts, toks), F32)
    for j in range(choices):
        chosen_t += jnp.where(idst[j:j + 1, :] == lane_e, 1.0, 0.0)
    chosen = jnp.transpose(chosen_t)[:, :experts]
    before = (iota((toks, toks), 0) > iota((toks, toks), 1)).astype(F32).astype(BF16)
    rank = mm(before, chosen.astype(BF16))
    rank_b = jnp.where(chosen > 0.0, rank, -1.0).astype(BF16)
    x = x_ref[...].astype(F32)
    x_inv = inv_rms(x)
    a = (x * x_inv).astype(BF16)

    for copy in own_w:
        copy.wait()
    pl.semaphore_wait(sem, len(peers))
    quarter = toks // 4
    two = ((0, 0, 2), (1, 2, 2))
    w_steps = gather_steps(place, sems, lambda d, lo, num: w_full.at[pl.ds(lo, num), rows_of(d)], 4, False, two)
    ids_steps = gather_steps(place, sems, lambda d, lo, num: ids_all.at[d], 1, False, ((0, 0, 1),))
    dy_steps = gather_steps(place, sems, lambda d, lo, num: dy_all.at[d, pl.ds(lo * quarter, num * quarter)], 4, True, two)
    for _ in range(4):
        next(w_steps)
    next(ids_steps)
    next(dy_steps)
    for i in range(4):
        next(w_steps)
        next(ids_steps)
        next(dy_steps, None)
    finish(w_steps)

    q_s[...] = mm(a, w_full[0]).astype(BF16)
    k_s[...] = mm(a, w_full[1]).astype(BF16)
    v_s[...] = mm(a, w_full[2]).astype(BF16)
    next(dy_steps, None)
    causal = iota((toks, toks), 0) >= iota((toks, toks), 1)
    low = iota((toks, 2 * HEAD_DIM), 1) < HEAD_DIM
    zero_b = jnp.zeros((toks, 2 * HEAD_DIM), BF16)
    pairs = d_model // (2 * HEAD_DIM)
    scale = HEAD_DIM ** -0.5

    def half(v, side):
        return jnp.where(low, v, zero_b) if side == 0 else jnp.where(low, zero_b, v)

    for pair in range(pairs):
        lanes = pl.ds(pair * 2 * HEAD_DIM, 2 * HEAD_DIM)
        qp, kp, vp = q_s[:, lanes], k_s[:, lanes], v_s[:, lanes]
        outs = []
        for side in range(2):
            s = jnp.where(causal, mm(half(qp, side), kp, NT) * scale, -1e30)
            e = jnp.exp(s - jnp.max(s, axis=-1, keepdims=True))
            p = e / jnp.sum(e, axis=-1, keepdims=True)
            prob_s[2 * pair + side] = p
            outs.append(mm(p.astype(BF16), vp))
        o_s[:, lanes] = jnp.where(low, outs[0], outs[1]).astype(BF16)
        next(dy_steps, None)
        next(ids_steps, None)

    hid = (x + mm(o_s[...], w_full[3])).astype(BF16)
    hid_s[...] = hid
    h = hid.astype(F32)
    h_inv = inv_rms(h)
    n = h * h_inv
    u_all[me] = n.astype(BF16)
    logits = mm(n, wr_ref[...], precision=EXACT)
    top = jnp.max(jnp.where(chosen > 0.0, logits, -3e38), axis=-1, keepdims=True)
    expd = jnp.where(chosen > 0.0, jnp.exp(logits - top), 0.0)
    gates = expd / jnp.sum(expd, axis=-1, keepdims=True)
    gates_t = jnp.transpose(jnp.concatenate([gates, jnp.zeros_like(gates)], axis=-1))
    for j in range(choices):
        g_all[me, j:j + 1, :] = jnp.sum(jnp.where(idst[j:j + 1, :] == lane_e, gates_t, 0.0), axis=0, keepdims=True)

    u_steps = gather_steps(place, sems, lambda d, lo, num: u_all.at[d, pl.ds(lo * quarter, num * quarter)], 4, True, two)
    g_steps = gather_steps(place, sems, lambda d, lo, num: g_all.at[d], 1, False, ((0, 0, 1),))
    next(u_steps)
    next(g_steps)
    finish(ids_steps)

    first_e = (me * local).astype(F32)
    row8 = iota((8, toks), 0)

    def find(i, _):
        ids = ids_all[place.at(*block_offset(i, place))]
        m = jnp.zeros((8, toks), F32)
        for e in range(local):
            hit = jnp.sum(jnp.where(ids == first_e + e, 1.0, 0.0), axis=0, keepdims=True)
            m = jnp.where(row8 == e, hit, m)
        m_s[i] = m
        return 0

    lax.fori_loop(0, group, find, 0)
    next(u_steps)
    next(g_steps, None)
    m_flat = m_s[...].reshape(group * 8, toks)
    after = (iota((toks, toks), 0) < iota((toks, toks), 1)).astype(F32).astype(BF16)
    r_flat = jnp.where(m_flat > 0.0, mm(m_flat.astype(BF16), after), -1.0)
    r_s[...] = r_flat.reshape(group, 8, toks)
    next(u_steps)
    next(g_steps, None)
    slot = iota((cap, toks), 0).astype(F32)

    def build(i, _):
        r = r_s[i]
        for e in range(local):
            pick_s[i, pl.ds(e * cap, cap), :] = jnp.where(slot == r[e:e + 1, :], 1.0, 0.0).astype(BF16)
        return 0

    lax.fori_loop(0, group, build, 0)
    next(u_steps)
    next(g_steps, None)
    finish(dy_steps)

    def take_rows(i, source, dest):
        rows = mm(pick_s[i], source[place.at(*block_offset(i, place))]).astype(BF16)
        for e in range(local):
            dest[e, pl.ds(pl.multiple_of(i * cap, cap), cap), :] = rows[e * cap:(e + 1) * cap]

    def take_dy(i, _):
        take_rows(i, dy_all, rdy_s)
        return 0

    lax.fori_loop(0, group // 2, take_dy, 0)
    next(u_steps)
    next(g_steps, None)
    lax.fori_loop(group // 2, group, take_dy, 0)
    finish(u_steps, g_steps)
    for copy in sems.sent:
        copy.wait_send()
    sems.sent = []

    z_base = sems.used
    sems.used += 2 * group
    d_base = z_base + group
    span = per * cap

    def outgoing(part, i):
        return dy_all.at[i, pl.ds(part * local * cap, local * cap)]

    def ship(part, i, back, base):
        target = place.at(*block_offset(i, place))
        return remote(outgoing(part, i), back.at[me], base + i, target, ssem, rsem)

    def put(part, e, g, rows):
        for b in range(per):
            dy_all[g * per + b, pl.ds((part * local + e) * cap, cap), :] = rows[b * cap:(b + 1) * cap]

    def start_group(part, g, back, base):
        @pl.when(g > 0)
        def _():
            ship(part, g * per, back, base).start()

        @pl.when(g == 0)
        def _():
            back[me] = outgoing(part, 0)[...]
        for b in range(1, per):
            ship(part, g * per + b, back, base).start()

    def forward(g, _):
        for b in range(per):
            take_rows(g * per + b, u_all, ru_s)
        rows = pl.ds(pl.multiple_of(g * span, span), span)
        for e in range(local):
            ru = ru_s[e, rows, :]
            ag = mm(ru, wg_ref[e])
            au = mm(ru, wu_ref[e])
            mid = (ag * jax.nn.sigmoid(ag) * au).astype(BF16)
            ag_s[e, rows, :] = ag
            au_s[e, rows, :] = au
            mid_s[e, rows, :] = mid
            put(0, e, g, mm(mid, wd_ref[e]).astype(BF16))
        start_group(0, g, zback, z_base)
        return 0

    lax.fori_loop(0, groups, forward, 0)

    def backward(g, _):
        for b in range(per):
            i = g * per + b
            d = place.at(*block_offset(i, place))
            ids, gts = ids_all[d], g_all[d]
            for e in range(local):
                gate = jnp.sum(jnp.where(ids == first_e + e, gts, 0.0), axis=0, keepdims=True)
                col = jnp.sum(pick_s[i, pl.ds(e * cap, cap), :].astype(F32) * gate, axis=-1, keepdims=True)
                at = pl.ds(pl.multiple_of(i * cap, cap), cap)
                rdy_s[e, at, :] = (col * rdy_s[e, at, :].astype(F32)).astype(BF16)
        rows = pl.ds(pl.multiple_of(g * span, span), span)
        for e in range(local):
            gm = mm(rdy_s[e, rows, :], wd_ref[e], NT)
            ag, au = ag_s[e, rows, :], au_s[e, rows, :]
            sg = jax.nn.sigmoid(ag)
            dag = (gm * au * sg * (1.0 + ag * (1.0 - sg))).astype(BF16)
            dau = (gm * ag * sg).astype(BF16)
            dag_s[e, rows, :] = dag
            dau_s[e, rows, :] = dau
            put(1, e, g, (mm(dag, wg_ref[e], NT) + mm(dau, wu_ref[e], NT)).astype(BF16))
        start_group(1, g, dback, d_base)
        return 0

    lax.fori_loop(0, groups, backward, 0)

    def weights(e, _):
        gd_ref[e] = mm(mid_s[e], rdy_s[e], TN).astype(BF16)
        gg_ref[e] = mm(ru_s[e], dag_s[e], TN).astype(BF16)
        gu_ref[e] = mm(ru_s[e], dau_s[e], TN).astype(BF16)
        return 0

    lax.fori_loop(0, local, weights, 0)

    def arrived(part, back, base):
        def one(i, _):
            dy_, dx_, dc_ = block_offset(i, place)
            origin = place.at(-dy_, -dx_, dc_)
            remote(back.at[origin], back.at[origin], base + i, origin, ssem, rsem).wait_recv()
            return 0
        lax.fori_loop(1, group, one, 0)

    wide = per * local * cap
    col = iota((1, wide), 1)
    colmod = col
    for _ in range(1, per * local):
        colmod = jnp.where(colmod >= cap, colmod - cap, colmod)
    colmod = colmod.astype(F32)
    g3 = three(gates)
    dyv = dy_ref[...]
    e_row, e_col = iota((experts, wide), 0), iota((experts, wide), 1)

    def combine(c, carry):
        y_sum, gg_sum = carry
        base = (e_row - c * per * local) * cap
        spread = jnp.where((e_col >= base) & (e_col < base + cap), 1.0, 0.0).astype(BF16)
        z = zback[pl.ds(c * per, per)].reshape(wide, d_model)
        here = mm(rank_b, spread) == colmod
        place_s[c] = jnp.where(here, 1.0, 0.0).astype(BF16)
        for piece in g3:
            y_sum += mm(jnp.where(here, mm(piece, spread), 0.0).astype(BF16), z)
        for piece in three(jnp.where(here, mm(dyv, z, NT), 0.0)):
            gg_sum += mm(piece, spread, NT)
        return y_sum, gg_sum

    arrived(0, zback, z_base)
    y_sum, g_gates = lax.fori_loop(0, groups, combine, (jnp.zeros((toks, d_model), F32), jnp.zeros((toks, experts), F32)))
    y_ref[...] = (hid_s[...].astype(F32) + y_sum).astype(BF16)
    g_logits = gates * (g_gates - jnp.sum(gates * g_gates, axis=-1, keepdims=True))
    g_hnorm = mm(g_logits, wr_ref[...], NT, EXACT)

    arrived(1, dback, d_base)
    gn = g_hnorm
    for c in range(groups):
        gn += mm(place_s[c], dback[c * per:(c + 1) * per].reshape(wide, d_model))
    h = hid_s[...].astype(F32)
    h_inv = inv_rms(h)
    g_hid = (dyv.astype(F32) + rms_back(h, h_inv, gn)).astype(BF16)
    o_s[...] = mm(g_hid, w_full[3], NT).astype(BF16)
    g_xn = jnp.zeros((toks, d_model), F32)
    for pair in range(pairs):
        lanes = pl.ds(pair * 2 * HEAD_DIM, 2 * HEAD_DIM)
        qp, kp, vp, dop = q_s[:, lanes], k_s[:, lanes], v_s[:, lanes], o_s[:, lanes]
        dq, dk, dv = [], [], []
        for side in range(2):
            p = prob_s[2 * pair + side]
            dp = mm(half(dop, side), vp, NT)
            ds = (p * (dp - jnp.sum(dp * p, axis=-1, keepdims=True)) * scale).astype(BF16)
            dq.append(mm(ds, kp))
            dk.append(mm(ds, qp, TN))
            dv.append(mm(p.astype(BF16), dop, TN))
        for i, parts in enumerate((dq, dk, dv)):
            grad = jnp.where(low, parts[0], parts[1]).astype(BF16)
            g_xn += mm(grad, w_full[i, :, lanes], NT)
    x = x_ref[...].astype(F32)
    gx_ref[...] = (g_hid.astype(F32) + rms_back(x, inv_rms(x), g_xn)).astype(BF16)

    def sent(i, _):
        ship(0, i, zback, z_base).wait_send()
        ship(1, i, dback, d_base).wait_send()
        return 0

    lax.fori_loop(1, group, sent, 0)


def solution(mesh):
    group = mesh.shape[AXIS]
    tok_spec = P(('dp', 'ep'), None)
    fsdp_spec = P('ep', None)
    expert_spec = P('ep', None, None)
    grad_spec = P(('dp', 'ep'), None, None)

    def device_step(x_tokens, expert_ids, grad_y, w_q, w_k, w_v, w_o, w_router, w_gate, w_up, w_down):
        toks, d_model = x_tokens.shape
        choices = expert_ids.shape[1]
        experts = w_router.shape[1]
        local, _, ff = w_gate.shape
        avg_load = toks * choices // experts
        cap = avg_load + avg_load // 2
        assert toks == SEQ_LEN
        heads = w_q.shape[1] // HEAD_DIM
        shape, vm = jax.ShapeDtypeStruct, pltpu.VMEM
        rows = group * cap
        per = 2 * math.isqrt(group // 2)
        in_vmem = pl.BlockSpec(memory_space=pltpu.VMEM)
        in_hbm = pl.BlockSpec(memory_space=pl.ANY)
        n_sem = 62 + 31 + 84 + 84 + 31 + 2 * group
        square = vm((toks, d_model), BF16)
        return pl.pallas_call(
            functools.partial(layer_kernel, group, experts, cap),
            out_shape=[shape(x_tokens.shape, BF16), shape(x_tokens.shape, BF16), shape(w_gate.shape, BF16),
                       shape(w_up.shape, BF16), shape(w_down.shape, BF16)],
            in_specs=[in_vmem] * 3 + [in_hbm] * 4 + [in_vmem] * 4,
            out_specs=[in_vmem] * 5,
            scratch_shapes=[
                vm((4, group * w_q.shape[0], d_model), BF16), vm((group, toks, d_model), BF16), vm((group, toks, d_model), BF16),
                vm((group, choices, toks), F32), vm((group, choices, toks), F32), vm((group, 8, toks), F32), vm((group, 8, toks), F32),
                vm((group, local * cap, toks), BF16), vm((local, rows, d_model), BF16), vm((local, rows, d_model), BF16),
                vm((local, rows, ff), F32), vm((local, rows, ff), F32),
                vm((local, rows, ff), BF16), vm((local, rows, ff), BF16), vm((local, rows, ff), BF16),
                vm((group, local * cap, d_model), BF16), vm((group, local * cap, d_model), BF16),
                vm((heads, toks, toks), F32), square, square, square, square, square,
                vm((group // per, toks, per * local * cap), BF16),
                pltpu.SemaphoreType.DMA((4,)), pltpu.SemaphoreType.DMA((n_sem,)), pltpu.SemaphoreType.DMA((n_sem,))],
            compiler_params=pltpu.CompilerParams(collective_id=1, has_side_effects=True, vmem_limit_bytes=67043328),
            name='layer')(x_tokens, expert_ids.T, grad_y, w_q, w_k, w_v, w_o, w_router, w_gate, w_up, w_down)

    return jax.shard_map(
        device_step, mesh=mesh,
        in_specs=(tok_spec, tok_spec, tok_spec, fsdp_spec, fsdp_spec, fsdp_spec, fsdp_spec,
                  P(None, None), expert_spec, expert_spec, expert_spec),
        out_specs=(tok_spec, tok_spec, grad_spec, grad_spec, grad_spec),
        check_vma=False)
```

time: 256 us -> 187 us (0.73); the launches traced: 252 us -> 186 us
  matrix products: 63.4 us -> 0 us
  Pallas kernels: 169 us -> 178 us
  other arithmetic: 8.4 us -> 0 us
    dot_general x33 -> x0, matrix products: 61.2 us -> none  [the longest x4 24.1 us: mm(): return lax.dot_general(a, b, dims, preferred_element_type=F32)]
    pallas_call x3 -> x1, Pallas kernels: 169 us -> 178 us  [device_step(): pl.pallas_call(functools.partial(layer_kernel, group, experts, cap), out_...]
    unnamed x42 -> x14, local copies, waits for them, and re-layouts: 2.05 us -> 7.44 us
    convert_element_type x6 -> x0, local copies, waits for them, and re-layouts: 5.38 us -> none  [the longest x1 2 us: device_step(): jnp.einsum('secf,efd->secd', mid_act, w_down, preferred_element_type=F32)]
    convert_element_type x5 -> x0, other arithmetic: 3.69 us -> none  [the longest x1 1.77 us: local_attention(): jax.nn.softmax(jnp.where(causal, scores, -1e+30), axis=-1).astype(BF16)]
where the time goes in v2:
time: 187 us; the launch traced here: 186 us
  Pallas kernels  178 us (95%)
  local copies, waits for them, and re-layouts  7.44 us (4%)
    pallas_call x1, Pallas kernels, device_step(): pl.pallas_call(functools.partial(layer_kernel, group, experts, cap), out_...  178 us
    unnamed x14, local copies, waits for them, and re-layouts  7.44 us

profile of v2, /device:TPU:97, one launch (start us, length us, event | category | flops | bytes accessed | tf_op | source)
XLA Modules:
  0.0 185.7 jit_solution(10139868088705296714)
XLA Ops:
  0.6 1.7 copy.16.wr_ref
  2.4 177.6 %layer.1 = (bf16[256,512]{1,0:T(8,128)(2,1)}, bf16[256,512]{1,0:T(8,128)(2,1)}, bf16[2,512,256]{2,1,0:T(8,128)(2,1)}, bf16[2,512,256]{2,1,0:T(8,128)(2,1)}, bf16[2,256,512]{2,1,0:T(8,128)(2,1)}) custom-call(bf16[256,512]{1,0:T(8,128)(2,1)} %x_ref.1, s32[8,256]{1,0:T(8,128)} %bitcast.1, bf16[256,512]{1,0:T(8,128)(2,1)} %dy_ref.1, bf16[16,512]{1,0:T(8,128)(2,1)} %wq_ref.1, ...), custom_call_target="tpu_custom_call" | custom-call | tf_op jit(solution)/shard_map/layer/pallas_call | solution.py:519
  180.0 0.0 copy-start.3
  180.0 0.0 copy-start.2
  180.0 1.7 copy.22
  181.8 0.0 copy-done.3
  181.8 0.7 copy.23
  182.5 0.0 copy-done.2
  182.5 0.0 copy-start.1
  182.5 0.8 copy.24
  183.3 0.4 copy-done.1
  183.7 0.0 copy-start
  183.7 0.8 copy.25
  184.5 0.4 copy-done
  184.9 0.8 copy.26
Async XLA Ops:
  180.0 1.8 copy-start.3
  180.0 2.5 %copy-start.2 = (bf16[2,512,256]{2,1,0:T(8,128)(2,1)S(1)}, bf16[2,512,256]{2,1,0:T(8,128)(2,1)}, u32[]{:S(2)}) copy-start(bf16[2,512,256]{2,1,0:T(8,128)(2,1)} %get-tuple-element.12) | copy-start | bytes 1572868
  182.5 1.2 copy-start.1
  183.7 1.2 copy-start

commit v3 on v2

v3 whole, which is shorter than its diff:
```python
import functools
import math

import jax
import jax.numpy as jnp
from jax import lax
from jax.experimental import pallas as pl
from jax.experimental.pallas import tpu as pltpu
from jax.sharding import PartitionSpec as P

NORM_EPS = 1e-6
SEQ_LEN = 256
HEAD_DIM = 64
AXIS = 'ep'
N_SEND = 9
N_RECV = 109
F32 = jnp.float32
BF16 = jnp.bfloat16


class Place:
    def __init__(self, group):
        self.group = group
        self.side = math.isqrt(group // 2)
        self.me = lax.axis_index(AXIS)
        self.core = lax.rem(self.me, 2)
        self.x = lax.rem(self.me // 2, self.side)
        self.y = self.me // (2 * self.side)

    def wrap(self, v):
        return lax.rem(v + self.side, self.side)

    def at(self, dy, dx, dc=0):
        return (self.wrap(self.y + dy) * self.side + self.wrap(self.x + dx)) * 2 + lax.rem(self.core + dc, 2)


def near_peers(pl_):
    return [pl_.at(0, 1), pl_.at(0, -1), pl_.at(1, 0), pl_.at(-1, 0), pl_.at(0, 2), pl_.at(2, 0), pl_.at(0, 0, 1)]


class Sems:
    def __init__(self, ssem, rsem):
        self.ssem, self.rsem, self.n_send, self.n_recv = ssem, rsem, 0, 0

    def new_send(self):
        self.n_send += 1
        return self.n_send - 1

    def new_recv(self, count=1):
        self.n_recv += count
        return self.n_recv - count

    def copy(self, src, dst, ks, kr, target):
        return pltpu.make_async_remote_copy(
            src_ref=src, dst_ref=dst, send_sem=self.ssem.at[ks], recv_sem=self.rsem.at[kr],
            device_id={AXIS: target}, device_id_type=pl.DeviceIdType.MESH)


def gather_steps(place, sems, region, most, relay, halves, merge=False):
    partner = place.at(0, 0, 1)
    chips = place.side * place.side
    ks, k_pass = sems.new_send(), sems.new_recv()
    k_second = sems.new_recv() if merge else None

    def dev(h, a, b, dc=0):
        return place.at(b, a, dc) if h == 0 else place.at(a, b, dc)

    def send(h, a, b, lo, num, target, kr=None):
        where = region(dev(h, a, b), lo, num)
        kr = sems.new_recv() if kr is None else kr
        sems.copy(where, where, ks, kr, target).start()
        return kr

    def wait(kr, h, a, b, lo, num):
        where = region(dev(h, a, b), lo, num)
        sems.copy(where, where, ks, kr, partner).wait_recv()

    def wait_most(kr, n):
        sems.copy(most(n), most(n), ks, kr, partner).wait_recv()

    def pass_on(h, a, b, lo, num):
        send(h, a, b, lo, num, partner, k_pass)

    first, second, rel1, rel2 = {}, {}, {}, {}
    shifts = (1, -1) if relay else (1, -1, 2)

    def go_second(h, a, lo, num):
        for s in shifts:
            second[h, a, s] = send(h, a, 0, lo, num, dev(h, 0, s), k_second)

    for h, lo, num in halves:
        for s in shifts:
            first[h, s] = send(h, 0, 0, lo, num, dev(h, s, 0))
    for h, lo, num in halves:
        go_second(h, 0, lo, num)
    for h, lo, num in halves:
        pass_on(h, 0, 0, lo, num)
    yield
    if not relay:
        for s in shifts:
            for h, lo, num in halves:
                wait(first[h, s], h, -s, 0, lo, num)
                go_second(h, -s, lo, num)
                pass_on(h, -s, 0, lo, num)
            yield
        if merge:
            wait_most(k_second, chips - place.side)
        for a in (0, -1, 1, -2):
            for s in shifts:
                for h, lo, num in halves:
                    if not merge:
                        wait(second[h, a, s], h, a, -s, lo, num)
                    pass_on(h, a, -s, lo, num)
            yield
    else:
        def relay_on(kr, h, a, b, lo, s, ta, tb):
            part = lo + (s == -1)
            return send(h, a, b, part, 1, dev(h, ta, tb), kr)

        for s in shifts:
            for h, lo, num in halves:
                wait(first[h, s], h, -s, 0, lo, num)
                rel1[h] = relay_on(rel1.get(h), h, -s, 0, lo, s, s, 0)
                go_second(h, -s, lo, num)
                pass_on(h, -s, 0, lo, num)
            yield

        def relay2(h, lo, num, a, s):
            wait(second[h, a, s], h, a, -s, lo, num)
            rel2[h, a] = relay_on(rel2.get((h, a)), h, a, -s, lo, s, 0, s)
            pass_on(h, a, -s, lo, num)

        for h, lo, num in halves:
            for s in shifts:
                relay2(h, lo, num, 0, s)
        yield
        for h, lo, num in halves:
            wait(rel1[h], h, 2, 0, lo, num)
            go_second(h, 2, lo, num)
            pass_on(h, 2, 0, lo, num)
        yield
        for a in (-1, 1, 2):
            for s in shifts:
                for h, lo, num in halves:
                    relay2(h, lo, num, a, s)
            yield
        for a in (0, -1, 1, 2):
            for h, lo, num in halves:
                wait(rel2[h, a], h, a, 2, lo, num)
                pass_on(h, a, 2, lo, num)
            yield
    wait_most(k_pass, chips)
    yield
    sems.copy(most(2 * chips - 1), most(2 * chips - 1), ks, k_pass, partner).wait_send()
    yield


def finish(*gens):
    gens = list(gens)
    while gens:
        gens = [g for g in gens if next(g, gens) is not gens]


NN = (((1,), (0,)), ((), ()))
NT = (((1,), (1,)), ((), ()))
TN = (((0,), (0,)), ((), ()))
EXACT = lax.Precision.HIGHEST


def mm(a, b, dims=NN, precision=None):
    return lax.dot_general(a, b, dims, precision=precision, preferred_element_type=F32)


def three(v):
    a = v.astype(BF16)
    v = v - a.astype(F32)
    b = v.astype(BF16)
    return a, b, (v - b.astype(F32)).astype(BF16)


def iota(shape, dim):
    return lax.broadcasted_iota(jnp.int32, shape, dim)


def inv_rms(v):
    return lax.rsqrt(jnp.mean(v * v, axis=-1, keepdims=True) + NORM_EPS)


def rms_back(v, inv, g):
    return inv * g - v * (inv * inv * inv * jnp.mean(g * v, axis=-1, keepdims=True))


def block_offset(i, side):
    return lax.rem(i // 2, side), i // (2 * side), lax.rem(i, 2)


def block_place(i, e, side):
    dy, dx, dc = block_offset(i, side)
    return i if e == 0 else (dy * side + dx) * 2 + dc


def layer_kernel(group, experts, cap, x_ref, idst_ref, dy_ref, wq_ref, wk_ref, wv_ref, wo_ref, wr_ref, wg_in, wu_in, wd_in,
                 y_ref, gx_ref, gg_ref, gu_ref, gd_ref,
                 w_full, u_all, dy_all, ids_all, g_all, m_s, r_s, pick_s, ru_s, rdy_s, ag_s, au_s, mid_s, dag_s, dau_s,
                 wg_ref, wu_ref, wd_ref, relay, zback, dback, prob_s, q_s, k_s, v_s, o_s, hid_s, place_s, gg_s, gu_s, gd_s, y_s,
                 lsem, ssem, rsem):
    place = Place(group)
    me = place.me
    toks, d_model = x_ref.shape
    choices = idst_ref.shape[0]
    local, _, ff = wg_in.shape
    depth = wq_ref.shape[0]
    per = 2 * place.side
    groups = group // per
    sems = Sems(ssem, rsem)

    def rows_of(d):
        return pl.ds(pl.multiple_of(d * depth, depth), depth)

    own_w = [pltpu.make_async_copy(w, w_full.at[i, rows_of(me)], lsem.at[i]) for i, w in enumerate((wq_ref, wk_ref, wv_ref, wo_ref))]
    experts_in = [pltpu.make_async_copy(src, dst, lsem.at[4 + i])
                  for i, (src, dst) in enumerate(((wg_in, wg_ref), (wu_in, wu_ref), (wd_in, wd_ref)))]
    for copy in own_w + experts_in:
        copy.start()
    sem = pltpu.get_barrier_semaphore()
    peers = near_peers(place)
    for peer in peers:
        pl.semaphore_signal(sem, inc=1, device_id={AXIS: peer}, device_id_type=pl.DeviceIdType.MESH)

    dy_all[me] = dy_ref[...]
    idst = idst_ref[...].astype(F32)
    ids_all[me] = idst
    lane_e = iota((2 * experts, toks), 0).astype(F32)
    chosen_t = jnp.zeros((2 * experts, toks), F32)
    for j in range(choices):
        chosen_t += jnp.where(idst[j:j + 1, :] == lane_e, 1.0, 0.0)
    chosen = jnp.transpose(chosen_t)[:, :experts]
    before = (iota((toks, toks), 0) > iota((toks, toks), 1)).astype(F32).astype(BF16)
    rank = mm(before, chosen.astype(BF16))
    rank_b = jnp.where(chosen > 0.0, rank, -1.0).astype(BF16)
    x = x_ref[...].astype(F32)
    x_inv = inv_rms(x)
    a = (x * x_inv).astype(BF16)

    for copy in own_w:
        copy.wait()
    pl.semaphore_wait(sem, len(peers))
    quarter = toks // 4
    two = ((0, 0, 2), (1, 2, 2))
    w_steps = gather_steps(place, sems, lambda d, lo, num: w_full.at[pl.ds(lo, num), rows_of(d)],
                           lambda n: w_full.at[:, pl.ds(0, n * depth)], False, two)
    ids_steps = gather_steps(place, sems, lambda d, lo, num: ids_all.at[d], lambda n: ids_all.at[pl.ds(0, n)], False, ((0, 0, 1),), True)
    dy_steps = gather_steps(place, sems, lambda d, lo, num: dy_all.at[d, pl.ds(lo * quarter, num * quarter)],
                            lambda n: dy_all.at[pl.ds(0, n)], True, two)
    for _ in range(4):
        next(w_steps)
    next(dy_steps)
    finish(w_steps)
    next(ids_steps)

    q_s[...] = mm(a, w_full[0]).astype(BF16)
    k_s[...] = mm(a, w_full[1]).astype(BF16)
    v_s[...] = mm(a, w_full[2]).astype(BF16)
    next(dy_steps, None)
    causal = iota((toks, toks), 0) >= iota((toks, toks), 1)
    low = iota((toks, 2 * HEAD_DIM), 1) < HEAD_DIM
    zero_b = jnp.zeros((toks, 2 * HEAD_DIM), BF16)
    pairs = d_model // (2 * HEAD_DIM)
    scale = HEAD_DIM ** -0.5

    def half(v, side):
        return jnp.where(low, v, zero_b) if side == 0 else jnp.where(low, zero_b, v)

    for pair in range(pairs):
        lanes = pl.ds(pair * 2 * HEAD_DIM, 2 * HEAD_DIM)
        qp, kp, vp = q_s[:, lanes], k_s[:, lanes], v_s[:, lanes]
        outs = []
        for hf in range(2):
            s = jnp.where(causal, mm(half(qp, hf), kp, NT) * scale, -1e30)
            e = jnp.exp(s - jnp.max(s, axis=-1, keepdims=True))
            p = e / jnp.sum(e, axis=-1, keepdims=True)
            prob_s[2 * pair + hf] = p
            outs.append(mm(p.astype(BF16), vp))
        o_s[:, lanes] = jnp.where(low, outs[0], outs[1]).astype(BF16)
        next(dy_steps, None)
        next(ids_steps, None)

    hid = (x + mm(o_s[...], w_full[3])).astype(BF16)
    hid_s[...] = hid
    h = hid.astype(F32)
    h_inv = inv_rms(h)
    n = h * h_inv
    u_all[me] = n.astype(BF16)
    logits = mm(n, wr_ref[...], NT, EXACT)
    top = jnp.max(jnp.where(chosen > 0.0, logits, -3e38), axis=-1, keepdims=True)
    expd = jnp.where(chosen > 0.0, jnp.exp(logits - top), 0.0)
    gates = expd / jnp.sum(expd, axis=-1, keepdims=True)
    gates_t = jnp.transpose(jnp.concatenate([gates, jnp.zeros_like(gates)], axis=-1))
    for j in range(choices):
        g_all[me, j:j + 1, :] = jnp.sum(jnp.where(idst[j:j + 1, :] == lane_e, gates_t, 0.0), axis=0, keepdims=True)

    u_steps = gather_steps(place, sems, lambda d, lo, num: u_all.at[d, pl.ds(lo * quarter, num * quarter)],
                           lambda n: u_all.at[pl.ds(0, n)], True, two)
    g_steps = gather_steps(place, sems, lambda d, lo, num: g_all.at[d], lambda n: g_all.at[pl.ds(0, n)], False, ((0, 0, 1),), True)
    next(u_steps)
    next(g_steps)
    finish(ids_steps)

    first_e = (me * local).astype(F32)
    row8 = iota((8, toks), 0)

    def find(i, _):
        ids = ids_all[place.at(*block_offset(i, place.side))]
        m = jnp.zeros((8, toks), F32)
        for e in range(local):
            hit = jnp.sum(jnp.where(ids == first_e + e, 1.0, 0.0), axis=0, keepdims=True)
            m = jnp.where(row8 == e, hit, m)
        m_s[i] = m
        return 0

    lax.fori_loop(0, group, find, 0)
    next(u_steps)
    next(dy_steps, None)
    m_flat = m_s[...].reshape(group * 8, toks)
    after = (iota((toks, toks), 0) < iota((toks, toks), 1)).astype(F32).astype(BF16)
    r_flat = jnp.where(m_flat > 0.0, mm(m_flat.astype(BF16), after), -1.0)
    r_s[...] = r_flat.reshape(group, 8, toks)
    next(u_steps)
    next(dy_steps, None)
    next(g_steps, None)
    slot = iota((cap, toks), 0).astype(F32)

    def build(i, _):
        r = r_s[i]
        for e in range(local):
            pick_s[i, pl.ds(e * cap, cap), :] = jnp.where(slot == r[e:e + 1, :], 1.0, 0.0).astype(BF16)
        return 0

    lax.fori_loop(0, group, build, 0)

    def take_rows(i, source, dest):
        rows = mm(pick_s[i], source[place.at(*block_offset(i, place.side))]).astype(BF16)
        for e in range(local):
            at = block_place(i, e, place.side) * cap
            dest[e, pl.ds(pl.multiple_of(at, cap), cap), :] = rows[e * cap:(e + 1) * cap]

    def take_dy(g, _):
        for b in range(per):
            take_rows(g * per + b, dy_all, rdy_s)
        return 0

    while next(u_steps, place) is None:
        next(dy_steps, None)
        next(g_steps, None)
    for copy in experts_in:
        copy.wait()

    span = per * cap
    side = place.side

    def axis(e, d1, d2, dc):
        return place.at(d2, d1, dc) if e == 0 else place.at(d1, d2, dc)

    k_first = sems.new_recv(2 * local)
    k_second = sems.new_recv(2)
    k_sent = [(sems.new_send(), sems.new_send()) for _ in range(2)]

    def first_hop(part, e, d1):
        src = u_all.at[pl.ds(d1 * per, per), pl.ds((part * local + e) * cap, cap)]
        return sems.copy(src, relay.at[part, e, d1], k_sent[part][0], k_first + part * local + e, axis(e, d1, 0, 0))

    def first_done(part, e):
        at = relay.at[part, e, pl.ds(1, side - 1)]
        return sems.copy(at, at, k_sent[part][0], k_first + part * local + e, me)

    def second_hop(part, e, d2, dc):
        back = (zback, dback)[part]
        return sems.copy(relay.at[part, e, :, 2 * d2 + dc], back.at[e, d2, dc], k_sent[part][1], k_second + part,
                         axis(e, 0, d2, dc))

    def all_first(part):
        at = relay.at[part, :, pl.ds(1, side - 1)]
        return sems.copy(at, at, k_sent[part][0], k_second, me)

    def all_second(part):
        at = relay.at[part, :, :, pl.ds(0, per - 1)]
        return sems.copy(at, at, k_sent[part][1], k_second + part, me)

    ahead = [(d2, dc) for d2 in range(side) for dc in range(2)][1:]
    ahead.sort(key=lambda t: -min(t[0], side - t[0]))

    def pass_rows(part):
        for e in range(local):
            first_done(part, e).wait_recv()
            for d2, dc in ahead:
                second_hop(part, e, d2, dc).start()
        for e in range(local):
            (zback, dback)[part][e, 0, 0] = relay[part, e, :, 0]

    def put(part, e, g, rows):
        @pl.when(g > 0)
        def _():
            for b in range(per):
                u_all[g * per + b, pl.ds((part * local + e) * cap, cap), :] = rows[b * cap:(b + 1) * cap]
            first_hop(part, e, g).start()

        @pl.when(g == 0)
        def _():
            for b in range(per):
                relay[part, e, 0, b] = rows[b * cap:(b + 1) * cap]

    def take_u(g, _):
        for b in range(per):
            take_rows(g * per + b, u_all, ru_s)
        return 0

    lax.fori_loop(0, groups, take_u, 0)

    def forward(step, _):
        g = lax.rem(step + side // 2, side)
        rows = pl.ds(pl.multiple_of(g * span, span), span)
        for e in range(local):
            ru = ru_s[e, rows, :]
            ag = mm(ru, wg_ref[e])
            au = mm(ru, wu_ref[e])
            mid = (ag * jax.nn.sigmoid(ag) * au).astype(BF16)
            ag_s[e, rows, :] = ag
            au_s[e, rows, :] = au
            mid_s[e, rows, :] = mid
            put(0, e, g, mm(mid, wd_ref[e]).astype(BF16))
        return 0

    lax.fori_loop(0, groups, forward, 0)

    def weigh(q, _):
        for i in [q * side + b for b in range(side)]:
            d = place.at(*block_offset(i, side))
            ids, gts = ids_all[d], g_all[d]
            for e in range(local):
                gate = jnp.sum(jnp.where(ids == first_e + e, gts, 0.0), axis=0, keepdims=True)
                col = jnp.sum(pick_s[i, pl.ds(e * cap, cap), :].astype(F32) * gate, axis=-1, keepdims=True)
                at = pl.ds(pl.multiple_of(block_place(i, e, side) * cap, cap), cap)
                rdy_s[e, at, :] = (col * rdy_s[e, at, :].astype(F32)).astype(BF16)
        return 0

    finish(g_steps, dy_steps)
    lax.fori_loop(0, groups, take_dy, 0)
    lax.fori_loop(0, group // side, weigh, 0)

    def backward(step, _):
        g = lax.rem(step + side // 2, side)
        rows = pl.ds(pl.multiple_of(g * span, span), span)
        for e in range(local):
            gm = mm(rdy_s[e, rows, :], wd_ref[e], NT)
            ag, au = ag_s[e, rows, :], au_s[e, rows, :]
            sg = jax.nn.sigmoid(ag)
            dag = (gm * au * sg * (1.0 + ag * (1.0 - sg))).astype(BF16)
            dau = (gm * ag * sg).astype(BF16)
            dag_s[e, rows, :] = dag
            dau_s[e, rows, :] = dau
            put(1, e, g, (mm(dag, wg_ref[e], NT) + mm(dau, wu_ref[e], NT)).astype(BF16))
        return 0

    lax.fori_loop(0, groups, backward, 0)

    def weights(e, _):
        gd_s[e] = mm(mid_s[e], rdy_s[e], TN).astype(BF16)
        gg_s[e] = mm(ru_s[e], dag_s[e], TN).astype(BF16)
        gu_s[e] = mm(ru_s[e], dau_s[e], TN).astype(BF16)
        return 0

    lax.fori_loop(0, local, weights, 0)
    grads_out = [pltpu.make_async_copy(src, dst, lsem.at[i])
                 for i, (src, dst) in enumerate(((gg_s, gg_ref), (gu_s, gu_ref), (gd_s, gd_ref), (y_s, y_ref)))]
    for copy in grads_out[:3]:
        copy.start()

    wide = per * local * cap
    col = iota((1, wide), 1)
    colmod = col
    for _ in range(1, per * local):
        colmod = jnp.where(colmod >= cap, colmod - cap, colmod)
    colmod = colmod.astype(F32)
    g3 = three(gates)
    dyv = dy_ref[...]
    e_row = iota((experts, wide), 0).astype(F32)
    halves = group // per // local

    def combine(c, carry):
        y_sum, gg_sum = carry
        e, top = c // halves, lax.rem(c, halves) * (side // halves)
        owner = jnp.zeros((1, wide), F32)
        for k in range(wide // cap):
            d2, dc, d1 = top + k // per, (k // side) % 2, k % side
            dx, dy = jnp.where(e == 0, d1, d2), jnp.where(e == 0, d2, d1)
            of_block = (place.at(-dy, -dx, dc) * local + e).astype(F32)
            owner = jnp.where((col >= k * cap) & (col < (k + 1) * cap), of_block, owner)
        spread = jnp.where(e_row == owner, 1.0, 0.0).astype(BF16)
        z = zback[e, pl.ds(top, side // halves)].reshape(wide, d_model)
        here = mm(rank_b, spread) == colmod
        place_s[c] = jnp.where(here, 1.0, 0.0).astype(BF16)
        for piece in g3:
            y_sum += mm(jnp.where(here, mm(piece, spread), 0.0).astype(BF16), z)
        for piece in three(jnp.where(here, mm(dyv, z, NT), 0.0)):
            gg_sum += mm(piece, spread, NT)
        return y_sum, gg_sum

    pass_rows(0)
    pass_rows(1)
    all_second(0).wait_recv()
    y_sum, g_gates = lax.fori_loop(0, groups, combine, (jnp.zeros((toks, d_model), F32), jnp.zeros((toks, experts), F32)))
    y_s[...] = (hid_s[...].astype(F32) + y_sum).astype(BF16)
    g_logits = gates * (g_gates - jnp.sum(gates * g_gates, axis=-1, keepdims=True))
    g_hnorm = mm(g_logits, wr_ref[...], NN, EXACT)

    grads_out[3].start()
    all_second(1).wait_recv()
    gn = g_hnorm
    for c in range(groups):
        top = c % halves * (side // halves)
        gn += mm(place_s[c], dback[c // halves, top:top + side // halves].reshape(wide, d_model))
    h = hid_s[...].astype(F32)
    h_inv = inv_rms(h)
    g_hid = (dyv.astype(F32) + rms_back(h, h_inv, gn)).astype(BF16)
    o_s[...] = mm(g_hid, w_full[3], NT).astype(BF16)
    g_xn = jnp.zeros((toks, d_model), F32)
    for pair in range(pairs):
        lanes = pl.ds(pair * 2 * HEAD_DIM, 2 * HEAD_DIM)
        qp, kp, vp, dop = q_s[:, lanes], k_s[:, lanes], v_s[:, lanes], o_s[:, lanes]
        dq, dk, dv = [], [], []
        for hf in range(2):
            p = prob_s[2 * pair + hf]
            dp = mm(half(dop, hf), vp, NT)
            ds = (p * (dp - jnp.sum(dp * p, axis=-1, keepdims=True)) * scale).astype(BF16)
            dq.append(mm(ds, kp))
            dk.append(mm(ds, qp, TN))
            dv.append(mm(p.astype(BF16), dop, TN))
        for i, parts in enumerate((dq, dk, dv)):
            grad = jnp.where(low, parts[0], parts[1]).astype(BF16)
            g_xn += mm(grad, w_full[i, :, lanes], NT)
    x = x_ref[...].astype(F32)
    gx_ref[...] = (g_hid.astype(F32) + rms_back(x, inv_rms(x), g_xn)).astype(BF16)

    for copy in grads_out:
        copy.wait()
    for part in range(2):
        all_first(part).wait_send()
        all_second(part).wait_send()
    assert (sems.n_send, sems.n_recv) == (N_SEND, N_RECV), (sems.n_send, sems.n_recv)


def settle_kernel(*refs):
    n = (len(refs) - 2) // 3
    ins, outs, held, lsem, ssem = refs[:n], refs[n:2 * n], refs[2 * n:3 * n], refs[-2], refs[-1]
    loads = [pltpu.make_async_copy(a, h, lsem.at[i]) for i, (a, h) in enumerate(zip(ins, held))]
    stores = [pltpu.make_async_copy(h, o, ssem.at[i]) for i, (h, o) in enumerate(zip(held, outs))]
    for copy in loads:
        copy.start()
    for load, store in zip(loads, stores):
        load.wait()
        store.start()
    for copy in stores:
        copy.wait()


def settle(*arrays):
    n = len(arrays)
    hbm = pl.BlockSpec(memory_space=pl.ANY)
    return pl.pallas_call(
        settle_kernel, out_shape=[jax.ShapeDtypeStruct(a.shape, a.dtype) for a in arrays],
        in_specs=[hbm] * n, out_specs=[hbm] * n,
        scratch_shapes=[pltpu.VMEM(a.shape, a.dtype) for a in arrays] + [pltpu.SemaphoreType.DMA((n,))] * 2,
        name='settle')(*arrays)


def solution(mesh):
    group = mesh.shape[AXIS]
    tok_spec = P(('dp', 'ep'), None)
    fsdp_spec = P('ep', None)
    expert_spec = P('ep', None, None)
    grad_spec = P(('dp', 'ep'), None, None)

    def device_step(x_tokens, expert_ids, grad_y, w_q, w_k, w_v, w_o, w_router, w_gate, w_up, w_down):
        toks, d_model = x_tokens.shape
        choices = expert_ids.shape[1]
        experts = w_router.shape[1]
        local, _, ff = w_gate.shape
        avg_load = toks * choices // experts
        cap = avg_load + avg_load // 2
        assert toks == SEQ_LEN
        heads = w_q.shape[1] // HEAD_DIM
        shape, vm = jax.ShapeDtypeStruct, pltpu.VMEM
        rows = group * cap
        side = math.isqrt(group // 2)
        per = 2 * side
        hop = (side, per, cap, d_model)
        assert local == 2
        in_vmem = pl.BlockSpec(memory_space=pltpu.VMEM)
        in_hbm = pl.BlockSpec(memory_space=pl.ANY)
        square = vm((toks, d_model), BF16)
        outs = pl.pallas_call(
            functools.partial(layer_kernel, group, experts, cap),
            out_shape=[shape(x_tokens.shape, BF16), shape(x_tokens.shape, BF16), shape(w_gate.shape, BF16),
                       shape(w_up.shape, BF16), shape(w_down.shape, BF16)],
            in_specs=[in_vmem] * 3 + [in_hbm] * 4 + [in_vmem] + [in_hbm] * 3,
            out_specs=[in_hbm, in_vmem] + [in_hbm] * 3,
            scratch_shapes=[
                vm((4, group * w_q.shape[0], d_model), BF16), vm((group, toks, d_model), BF16), vm((group, toks, d_model), BF16),
                vm((group, choices, toks), F32), vm((group, choices, toks), F32), vm((group, 8, toks), F32), vm((group, 8, toks), F32),
                vm((group, local * cap, toks), BF16), vm((local, rows, d_model), BF16), vm((local, rows, d_model), BF16),
                vm((local, rows, ff), F32), vm((local, rows, ff), F32),
                vm((local, rows, ff), BF16), vm((local, rows, ff), BF16), vm((local, rows, ff), BF16),
                vm(w_gate.shape, BF16), vm(w_up.shape, BF16), vm(w_down.shape, BF16), vm((2, local) + hop, BF16),
                vm((local, side, 2, side, cap, d_model), BF16), vm((local, side, 2, side, cap, d_model), BF16),
                vm((heads, toks, toks), F32), square, square, square, square, square,
                vm((group // per, toks, per * local * cap), BF16),
                vm(w_gate.shape, BF16), vm(w_up.shape, BF16), vm(w_down.shape, BF16), square,
                pltpu.SemaphoreType.DMA((7,)), pltpu.SemaphoreType.DMA((N_SEND,)), pltpu.SemaphoreType.DMA((N_RECV,))],
            compiler_params=pltpu.CompilerParams(collective_id=1, has_side_effects=True, vmem_limit_bytes=67043328),
            name='layer')(x_tokens, expert_ids.T, grad_y, w_q, w_k, w_v, w_o, w_router.T, w_gate, w_up, w_down)
        return settle(*outs)

    return jax.shard_map(
        device_step, mesh=mesh,
        in_specs=(tok_spec, tok_spec, tok_spec, fsdp_spec, fsdp_spec, fsdp_spec, fsdp_spec,
                  P(None, None), expert_spec, expert_spec, expert_spec),
        out_specs=(tok_spec, tok_spec, grad_spec, grad_spec, grad_spec),
        check_vma=False)
```

time: 187 us -> 153 us (0.82)
  Pallas kernels: 178 us -> 152 us
  local copies, waits for them, and re-layouts: 7.44 us -> 0 us
    pallas_call x1, Pallas kernels: 178 us -> 150 us  [device_step(): pl.pallas_call(functools.partial(layer_kernel, group, experts, cap), out_...]
    unnamed x14 -> x0, local copies, waits for them, and re-layouts: 7.44 us -> none
    pallas_call x0 -> x1, Pallas kernels: none -> 2.43 us  [settle(): pl.pallas_call(settle_kernel, out_shape=[jax.ShapeDtypeStruct(a.shape, a....]
where the time goes in v3:
time: 153 us
  Pallas kernels  152 us (99%)
    pallas_call x1, Pallas kernels, device_step(): pl.pallas_call(functools.partial(layer_kernel, group, experts, cap), out_...  150 us

profile of v3, /device:TPU:97, one launch (start us, length us, event | category | flops | bytes accessed | tf_op | source)
XLA Modules:
  0.0 152.9 jit_solution(6410062552349517661)
XLA Ops:
  0.6 149.7 %layer.1 = (bf16[256,512]{1,0:T(8,128)(2,1)}, bf16[256,512]{1,0:T(8,128)(2,1)}, bf16[2,512,256]{2,1,0:T(8,128)(2,1)}, bf16[2,512,256]{2,1,0:T(8,128)(2,1)}, bf16[2,256,512]{2,1,0:T(8,128)(2,1)}) custom-call(bf16[256,512]{1,0:T(8,128)(2,1)} %x_ref.1, s32[8,256]{1,0:T(8,128)} %bitcast.3, bf16[256,512]{1,0:T(8,128)(2,1)} %dy_ref.1, bf16[16,512]{1,0:T(8,128)(2,1)} %wq_ref.1, ...), custom_call_target="tpu_custom_call" | custom-call | tf_op jit(solution)/shard_map/layer/pallas_call | solution.py:601
  150.3 2.4 %settle.1 = (bf16[256,512]{1,0:T(8,128)(2,1)}, bf16[256,512]{1,0:T(8,128)(2,1)}, bf16[2,512,256]{2,1,0:T(8,128)(2,1)}, bf16[2,512,256]{2,1,0:T(8,128)(2,1)}, bf16[2,256,512]{2,1,0:T(8,128)(2,1)}) custom-call(bf16[256,512]{1,0:T(8,128)(2,1)} %get-tuple-element.10.refs_0_, bf16[256,512]{1,0:T(8,128)(2,1)} %get-tuple-element.11.refs_1_, ...), custom_call_target="tpu_custom_call" | custom-call | tf_op jit(solution)/shard_map/settle/pallas_call | solution.py:569

commit v4 on v3

--- a/solution.py
+++ b/solution.py
@@ -12,8 +12,8 @@
 SEQ_LEN = 256
 HEAD_DIM = 64
 AXIS = 'ep'
-N_SEND = 9
-N_RECV = 109
+N_SEND = 10
+N_RECV = 110
 F32 = jnp.float32
 BF16 = jnp.bfloat16
 
@@ -190,19 +190,23 @@
     return inv * g - v * (inv * inv * inv * jnp.mean(g * v, axis=-1, keepdims=True))
 
 
-def block_offset(i, side):
-    return lax.rem(i // 2, side), i // (2 * side), lax.rem(i, 2)
-
-
-def block_place(i, e, side):
-    dy, dx, dc = block_offset(i, side)
-    return i if e == 0 else (dy * side + dx) * 2 + dc
+def turn(place, dest_core, d1, d2):
+    along_x = dest_core == 0
+    return jnp.where(along_x, d2, d1), jnp.where(along_x, d1, d2)
+
+
+def block_offset(i, place):
+    side = place.side
+    d1, dc = i // (2 * side), lax.rem(i // side, 2)
+    d2 = lax.rem(i // 2, 2) + 2 * lax.rem(i, 2)
+    dy, dx = turn(place, lax.rem(place.core + dc, 2), d1, d2)
+    return dy, dx, dc
 
 
 def layer_kernel(group, experts, cap, x_ref, idst_ref, dy_ref, wq_ref, wk_ref, wv_ref, wo_ref, wr_ref, wg_in, wu_in, wd_in,
                  y_ref, gx_ref, gg_ref, gu_ref, gd_ref,
                  w_full, u_all, dy_all, ids_all, g_all, m_s, r_s, pick_s, ru_s, rdy_s, ag_s, au_s, mid_s, dag_s, dau_s,
-                 wg_ref, wu_ref, wd_ref, relay, zback, dback, prob_s, q_s, k_s, v_s, o_s, hid_s, place_s, gg_s, gu_s, gd_s, y_s,
+                 wg_ref, wu_ref, wd_ref, relay, sums, total, small, smalls, prob_s, q_s, k_s, v_s, o_s, hid_s, place_s, gg_s, gu_s, gd_s, y_s,
                  lsem, ssem, rsem):
     place = Place(group)
     me = place.me
@@ -236,8 +240,6 @@
         chosen_t += jnp.where(idst[j:j + 1, :] == lane_e, 1.0, 0.0)
     chosen = jnp.transpose(chosen_t)[:, :experts]
     before = (iota((toks, toks), 0) > iota((toks, toks), 1)).astype(F32).astype(BF16)
-    rank = mm(before, chosen.astype(BF16))
-    rank_b = jnp.where(chosen > 0.0, rank, -1.0).astype(BF16)
     x = x_ref[...].astype(F32)
     x_inv = inv_rms(x)
     a = (x * x_inv).astype(BF16)
@@ -282,7 +284,8 @@
             prob_s[2 * pair + hf] = p
             outs.append(mm(p.astype(BF16), vp))
         o_s[:, lanes] = jnp.where(low, outs[0], outs[1]).astype(BF16)
-        next(dy_steps, None)
+        if pair >= 2:
+            next(dy_steps, None)
         next(ids_steps, None)
 
     hid = (x + mm(o_s[...], w_full[3])).astype(BF16)
@@ -310,7 +313,7 @@
     row8 = iota((8, toks), 0)
 
     def find(i, _):
-        ids = ids_all[place.at(*block_offset(i, place.side))]
+        ids = ids_all[place.at(*block_offset(i, place))]
         m = jnp.zeros((8, toks), F32)
         for e in range(local):
             hit = jnp.sum(jnp.where(ids == first_e + e, 1.0, 0.0), axis=0, keepdims=True)
@@ -339,9 +342,9 @@
     lax.fori_loop(0, group, build, 0)
 
     def take_rows(i, source, dest):
-        rows = mm(pick_s[i], source[place.at(*block_offset(i, place.side))]).astype(BF16)
+        rows = mm(pick_s[i], source[place.at(*block_offset(i, place))]).astype(BF16)
         for e in range(local):
-            at = block_place(i, e, place.side) * cap
+            at = i * cap
             dest[e, pl.ds(pl.multiple_of(at, cap), cap), :] = rows[e * cap:(e + 1) * cap]
 
     def take_dy(g, _):
@@ -357,57 +360,48 @@
 
     span = per * cap
     side = place.side
-
-    def axis(e, d1, d2, dc):
-        return place.at(d2, d1, dc) if e == 0 else place.at(d1, d2, dc)
-
-    k_first = sems.new_recv(2 * local)
-    k_second = sems.new_recv(2)
-    k_sent = [(sems.new_send(), sems.new_send()) for _ in range(2)]
-
-    def first_hop(part, e, d1):
-        src = u_all.at[pl.ds(d1 * per, per), pl.ds((part * local + e) * cap, cap)]
-        return sems.copy(src, relay.at[part, e, d1], k_sent[part][0], k_first + part * local + e, axis(e, d1, 0, 0))
-
-    def first_done(part, e):
-        at = relay.at[part, e, pl.ds(1, side - 1)]
-        return sems.copy(at, at, k_sent[part][0], k_first + part * local + e, me)
-
-    def second_hop(part, e, d2, dc):
-        back = (zback, dback)[part]
-        return sems.copy(relay.at[part, e, :, 2 * d2 + dc], back.at[e, d2, dc], k_sent[part][1], k_second + part,
-                         axis(e, 0, d2, dc))
-
-    def all_first(part):
-        at = relay.at[part, :, pl.ds(1, side - 1)]
-        return sems.copy(at, at, k_sent[part][0], k_second, me)
-
-    def all_second(part):
-        at = relay.at[part, :, :, pl.ds(0, per - 1)]
-        return sems.copy(at, at, k_sent[part][1], k_second + part, me)
-
-    ahead = [(d2, dc) for d2 in range(side) for dc in range(2)][1:]
-    ahead.sort(key=lambda t: -min(t[0], side - t[0]))
-
-    def pass_rows(part):
-        for e in range(local):
-            first_done(part, e).wait_recv()
-            for d2, dc in ahead:
-                second_hop(part, e, d2, dc).start()
-        for e in range(local):
-            (zback, dback)[part][e, 0, 0] = relay[part, e, :, 0]
+    both = local * cap
+    k_first, k_second, k_small = sems.new_recv(4), sems.new_recv(2), sems.new_recv()
+    k_rows, k_sums, k_smalls = [sems.new_send() for _ in range(2)], [sems.new_send() for _ in range(2)], sems.new_send()
+
+    def first_hop(part, d1, dc, p):
+        core = lax.rem(place.core + dc, 2)
+        relay_dc = (dc + p) % 2
+        src = u_all.at[pl.ds(d1 * per + dc * side + 2 * p, 2), pl.ds(part * both, both)]
+        return sems.copy(src, relay.at[part, p, :, 2 * d1 + relay_dc], k_rows[part], k_first + 2 * part + p,
+                         place.at(*turn(place, core, d1, 0), relay_dc))
+
+    def first_done(part, p):
+        at = relay.at[part, p, :, pl.ds(1, per - 1)]
+        return sems.copy(at, at, k_rows[part], k_first + 2 * part + p, me)
+
+    def dest_of(p, j):
+        core = lax.rem(place.core + p, 2)
+        return place.at(*turn(place, core, 0, p + 2 * j), p)
+
+    def second_hop(part, p, j):
+        return sems.copy(sums.at[part, 2 * j + p - 1], total.at[part, 2 * j + p], k_sums[part], k_second + part, dest_of(p, j))
+
+    def small_hop(p, j):
+        return sems.copy(small.at[2 * j + p - 1], smalls.at[2 * j + p], k_smalls, k_small, dest_of(p, j))
 
     def put(part, e, g, rows):
+        for b in range(per):
+            u_all[g * per + b, pl.ds(part * both + e * cap, cap), :] = rows[b * cap:(b + 1) * cap]
+
+    def start_group(part, g):
         @pl.when(g > 0)
         def _():
-            for b in range(per):
-                u_all[g * per + b, pl.ds((part * local + e) * cap, cap), :] = rows[b * cap:(b + 1) * cap]
-            first_hop(part, e, g).start()
+            for dc in range(2):
+                for p in range(2):
+                    first_hop(part, g, dc, p).start()
 
         @pl.when(g == 0)
         def _():
-            for b in range(per):
-                relay[part, e, 0, b] = rows[b * cap:(b + 1) * cap]
+            for p in range(2):
+                first_hop(part, 0, 1 - p, p).start()
+                for j in range(2):
+                    relay[part, p, j, 0] = u_all[p * side + 2 * p + j, pl.ds(part * both, both), :]
 
     def take_u(g, _):
         for b in range(per):
@@ -428,18 +422,19 @@
             au_s[e, rows, :] = au
             mid_s[e, rows, :] = mid
             put(0, e, g, mm(mid, wd_ref[e]).astype(BF16))
+        start_group(0, g)
         return 0
 
     lax.fori_loop(0, groups, forward, 0)
 
     def weigh(q, _):
         for i in [q * side + b for b in range(side)]:
-            d = place.at(*block_offset(i, side))
+            d = place.at(*block_offset(i, place))
             ids, gts = ids_all[d], g_all[d]
             for e in range(local):
                 gate = jnp.sum(jnp.where(ids == first_e + e, gts, 0.0), axis=0, keepdims=True)
                 col = jnp.sum(pick_s[i, pl.ds(e * cap, cap), :].astype(F32) * gate, axis=-1, keepdims=True)
-                at = pl.ds(pl.multiple_of(block_place(i, e, side) * cap, cap), cap)
+                at = pl.ds(pl.multiple_of(i * cap, cap), cap)
                 rdy_s[e, at, :] = (col * rdy_s[e, at, :].astype(F32)).astype(BF16)
         return 0
 
@@ -459,6 +454,7 @@
             dag_s[e, rows, :] = dag
             dau_s[e, rows, :] = dau
             put(1, e, g, (mm(dag, wg_ref[e], NT) + mm(dau, wu_ref[e], NT)).astype(BF16))
+        start_group(1, g)
         return 0
 
     lax.fori_loop(0, groups, backward, 0)
@@ -475,50 +471,104 @@
     for copy in grads_out[:3]:
         copy.start()
 
-    wide = per * local * cap
+    wide = per * both
+    blocks = wide // cap
     col = iota((1, wide), 1)
     colmod = col
-    for _ in range(1, per * local):
+    for _ in range(1, blocks):
         colmod = jnp.where(colmod >= cap, colmod - cap, colmod)
     colmod = colmod.astype(F32)
-    g3 = three(gates)
+    e_row = iota((experts, wide), 0).astype(F32)
+    blk = iota((blocks, wide), 0) * cap
+    blk_col = iota((blocks, wide), 1)
+    block_of = jnp.where((blk_col >= blk) & (blk_col < blk + cap), 1.0, 0.0).astype(BF16)
+
+    def owner_at(core, p, d1, dc, d2, e):
+        dy, dx = turn(place, core, -d1, -d2)
+        return (place.at(dy, dx, p + dc) * local + e).astype(F32)
+
+    def relay_z(q, _):
+        p, j = q % 2, q // 2
+        core = lax.rem(place.core + p, 2)
+        dest = dest_of(p, j)
+        owner = jnp.zeros((1, wide), F32)
+        for b in range(blocks):
+            s, e = b // local, b % local
+            owner = jnp.where((col >= b * cap) & (col < (b + 1) * cap), owner_at(core, 0, s // 2, s % 2, 0, e), owner)
+        spread = jnp.where(e_row == owner, 1.0, 0.0).astype(BF16)
+        ids, gts = ids_all[dest], g_all[dest]
+        e_in = iota((2 * experts, toks), 0)
+        e_id = jnp.where(e_in >= experts, e_in - experts, e_in).astype(F32)
+        both_t = jnp.zeros((2 * experts, toks), F32)
+        for c in range(choices):
+            both_t += jnp.where(ids[c:c + 1, :] == e_id, jnp.where(e_in >= experts, gts[c:c + 1, :], 1.0), 0.0)
+        both_v = jnp.transpose(both_t)
+        chose, weight = both_v[:, :experts], both_v[:, experts:]
+        ranks = jnp.where(chose > 0.0, mm(before, chose.astype(BF16)), -1.0).astype(BF16)
+        z = relay[0, p, j].reshape(wide, d_model)
+        here = mm(ranks, spread) == colmod
+        place_s[q] = jnp.where(here, 1.0, 0.0).astype(BF16)
+        y_sum = jnp.zeros((toks, d_model), F32)
+        for piece in three(weight):
+            y_sum += mm(jnp.where(here, mm(piece, spread), 0.0).astype(BF16), z)
+        gg_sum = jnp.zeros((blocks, toks), F32)
+        for piece in three(jnp.where(here, mm(dy_all[dest], z, NT), 0.0)):
+            gg_sum += mm(block_of, piece, NT)
+
+        @pl.when(q == 0)
+        def _():
+            total[0, 0] = y_sum
+            smalls[0] = gg_sum
+
+        @pl.when(q > 0)
+        def _():
+            sums[0, q - 1] = y_sum
+            small[q - 1] = gg_sum
+            second_hop(0, p, j).start()
+            small_hop(p, j).start()
+        return 0
+
+    for p in range(2):
+        first_done(0, p).wait_recv()
+    lax.fori_loop(0, side, lambda t, _: relay_z(lax.rem(t + 2, side), 0), 0)
+    for p in range(2):
+        first_done(1, p).wait_recv()
+
+    def relay_d(q, _):
+        p, j = q % 2, q // 2
+        sums_d = mm(place_s[q], relay[1, p, j].reshape(wide, d_model))
+
+        @pl.when(q == 0)
+        def _():
+            total[1, 0] = sums_d
+
+        @pl.when(q > 0)
+        def _():
+            sums[1, q - 1] = sums_d
+            second_hop(1, p, j).start()
+        return 0
+
+    lax.fori_loop(0, side, lambda t, _: relay_d(lax.rem(t + 2, side), 0), 0)
+
+    rest = pl.ds(1, side - 1)
+    sems.copy(total.at[0, rest], total.at[0, rest], k_sums[0], k_second, me).wait_recv()
+    sems.copy(smalls.at[rest], smalls.at[rest], k_smalls, k_small, me).wait_recv()
     dyv = dy_ref[...]
-    e_row = iota((experts, wide), 0).astype(F32)
-    halves = group // per // local
-
-    def combine(c, carry):
-        y_sum, gg_sum = carry
-        e, top = c // halves, lax.rem(c, halves) * (side // halves)
-        owner = jnp.zeros((1, wide), F32)
-        for k in range(wide // cap):
-            d2, dc, d1 = top + k // per, (k // side) % 2, k % side
-            dx, dy = jnp.where(e == 0, d1, d2), jnp.where(e == 0, d2, d1)
-            of_block = (place.at(-dy, -dx, dc) * local + e).astype(F32)
-            owner = jnp.where((col >= k * cap) & (col < (k + 1) * cap), of_block, owner)
-        spread = jnp.where(e_row == owner, 1.0, 0.0).astype(BF16)
-        z = zback[e, pl.ds(top, side // halves)].reshape(wide, d_model)
-        here = mm(rank_b, spread) == colmod
-        place_s[c] = jnp.where(here, 1.0, 0.0).astype(BF16)
-        for piece in g3:
-            y_sum += mm(jnp.where(here, mm(piece, spread), 0.0).astype(BF16), z)
-        for piece in three(jnp.where(here, mm(dyv, z, NT), 0.0)):
-            gg_sum += mm(piece, spread, NT)
-        return y_sum, gg_sum
-
-    pass_rows(0)
-    pass_rows(1)
-    all_second(0).wait_recv()
-    y_sum, g_gates = lax.fori_loop(0, groups, combine, (jnp.zeros((toks, d_model), F32), jnp.zeros((toks, experts), F32)))
-    y_s[...] = (hid_s[...].astype(F32) + y_sum).astype(BF16)
+    y_s[...] = (hid_s[...].astype(F32) + ((total[0, 0] + total[0, 1]) + (total[0, 2] + total[0, 3]))).astype(BF16)
+    grads_out[3].start()
+    m_col = iota((experts, 1), 0)
+    owner = jnp.zeros((experts, 1), F32)
+    for m in range(experts):
+        d2, s, e = m // blocks, (m % blocks) // local, m % local
+        owner = jnp.where(m_col == m, owner_at(place.core, d2 % 2, s // 2, s % 2, d2, e), owner)
+    perm = jnp.where(owner == iota((experts, experts), 1).astype(F32), 1.0, 0.0).astype(BF16)
+    g_gates = jnp.zeros((toks, experts), F32)
+    for piece in three(smalls[...].reshape(experts, toks)):
+        g_gates += mm(piece, perm, TN)
     g_logits = gates * (g_gates - jnp.sum(gates * g_gates, axis=-1, keepdims=True))
     g_hnorm = mm(g_logits, wr_ref[...], NN, EXACT)
-
-    grads_out[3].start()
-    all_second(1).wait_recv()
-    gn = g_hnorm
-    for c in range(groups):
-        top = c % halves * (side // halves)
-        gn += mm(place_s[c], dback[c // halves, top:top + side // halves].reshape(wide, d_model))
+    sems.copy(total.at[1, rest], total.at[1, rest], k_sums[1], k_second + 1, me).wait_recv()
+    gn = g_hnorm + ((total[1, 0] + total[1, 1]) + (total[1, 2] + total[1, 3]))
     h = hid_s[...].astype(F32)
     h_inv = inv_rms(h)
     g_hid = (dyv.astype(F32) + rms_back(h, h_inv, gn)).astype(BF16)
@@ -544,8 +594,10 @@
     for copy in grads_out:
         copy.wait()
     for part in range(2):
-        all_first(part).wait_send()
-        all_second(part).wait_send()
+        at = relay.at[part, :, :, pl.ds(1, per - 1)]
+        sems.copy(at, at, k_rows[part], k_first, me).wait_send()
+        sems.copy(sums.at[part], sums.at[part], k_sums[part], k_second, me).wait_send()
+    sems.copy(small, small, k_smalls, k_small, me).wait_send()
     assert (sems.n_send, sems.n_recv) == (N_SEND, N_RECV), (sems.n_send, sems.n_recv)
 
 
@@ -593,7 +645,6 @@
         rows = group * cap
         side = math.isqrt(group // 2)
         per = 2 * side
-        hop = (side, per, cap, d_model)
         assert local == 2
         in_vmem = pl.BlockSpec(memory_space=pltpu.VMEM)
         in_hbm = pl.BlockSpec(memory_space=pl.ANY)
@@ -610,8 +661,9 @@
                 vm((group, local * cap, toks), BF16), vm((local, rows, d_model), BF16), vm((local, rows, d_model), BF16),
                 vm((local, rows, ff), F32), vm((local, rows, ff), F32),
                 vm((local, rows, ff), BF16), vm((local, rows, ff), BF16), vm((local, rows, ff), BF16),
-                vm(w_gate.shape, BF16), vm(w_up.shape, BF16), vm(w_down.shape, BF16), vm((2, local) + hop, BF16),
-                vm((local, side, 2, side, cap, d_model), BF16), vm((local, side, 2, side, cap, d_model), BF16),
+                vm(w_gate.shape, BF16), vm(w_up.shape, BF16), vm(w_down.shape, BF16), vm((2, 2, 2, per, local * cap, d_model), BF16),
+                vm((2, side - 1, toks, d_model), F32), vm((2, side, toks, d_model), F32),
+                vm((side - 1, experts // side, toks), F32), vm((side, experts // side, toks), F32),
                 vm((heads, toks, toks), F32), square, square, square, square, square,
                 vm((group // per, toks, per * local * cap), BF16),
                 vm(w_gate.shape, BF16), vm(w_up.shape, BF16), vm(w_down.shape, BF16), square,

time: 153 us -> 141 us (0.922)
  Pallas kernels: 152 us -> 140 us
    pallas_call x1, Pallas kernels: 150 us -> 138 us  [device_step(): pl.pallas_call(functools.partial(layer_kernel, group, experts, cap), out_...]
where the time goes in v4:
time: 141 us
  Pallas kernels  140 us (99%)
    pallas_call x1, Pallas kernels, device_step(): pl.pallas_call(functools.partial(layer_kernel, group, experts, cap), out_...  138 us

profile of v4, /device:TPU:97, one launch (start us, length us, event | category | flops | bytes accessed | tf_op | source)
XLA Modules:
  0.0 140.8 jit_solution(3476116395535586898)
XLA Ops:
  0.6 137.5 %layer.1 = (bf16[256,512]{1,0:T(8,128)(2,1)}, bf16[256,512]{1,0:T(8,128)(2,1)}, bf16[2,512,256]{2,1,0:T(8,128)(2,1)}, bf16[2,512,256]{2,1,0:T(8,128)(2,1)}, bf16[2,256,512]{2,1,0:T(8,128)(2,1)}) custom-call(bf16[256,512]{1,0:T(8,128)(2,1)} %x_ref.1, s32[8,256]{1,0:T(8,128)} %bitcast.3, bf16[256,512]{1,0:T(8,128)(2,1)} %dy_ref.1, bf16[16,512]{1,0:T(8,128)(2,1)} %wq_ref.1, ...), custom_call_target="tpu_custom_call" | custom-call | tf_op jit(solution)/shard_map/layer/pallas_call | solution.py:652
  138.2 2.4 %settle.1 = (bf16[256,512]{1,0:T(8,128)(2,1)}, bf16[256,512]{1,0:T(8,128)(2,1)}, bf16[2,512,256]{2,1,0:T(8,128)(2,1)}, bf16[2,512,256]{2,1,0:T(8,128)(2,1)}, bf16[2,256,512]{2,1,0:T(8,128)(2,1)}) custom-call(bf16[256,512]{1,0:T(8,128)(2,1)} %get-tuple-element.10.refs_0_, bf16[256,512]{1,0:T(8,128)(2,1)} %get-tuple-element.11.refs_1_, ...), custom_call_target="tpu_custom_call" | custom-call | tf_op jit(solution)/shard_map/settle/pallas_call | solution.py:621

commit v5 on v4

--- a/solution.py
+++ b/solution.py
@@ -254,8 +254,13 @@
     ids_steps = gather_steps(place, sems, lambda d, lo, num: ids_all.at[d], lambda n: ids_all.at[pl.ds(0, n)], False, ((0, 0, 1),), True)
     dy_steps = gather_steps(place, sems, lambda d, lo, num: dy_all.at[d, pl.ds(lo * quarter, num * quarter)],
                             lambda n: dy_all.at[pl.ds(0, n)], True, two)
-    for _ in range(4):
+    next(w_steps)
+    next(ids_steps)
+    next(dy_steps)
+    for _ in range(3):
         next(w_steps)
+        next(ids_steps)
+    next(dy_steps)
     next(dy_steps)
     finish(w_steps)
     next(ids_steps)
@@ -284,9 +289,8 @@
             prob_s[2 * pair + hf] = p
             outs.append(mm(p.astype(BF16), vp))
         o_s[:, lanes] = jnp.where(low, outs[0], outs[1]).astype(BF16)
-        if pair >= 2:
+        if pair >= 3:
             next(dy_steps, None)
-        next(ids_steps, None)
 
     hid = (x + mm(o_s[...], w_full[3])).astype(BF16)
     hid_s[...] = hid
@@ -305,8 +309,8 @@
     u_steps = gather_steps(place, sems, lambda d, lo, num: u_all.at[d, pl.ds(lo * quarter, num * quarter)],
                            lambda n: u_all.at[pl.ds(0, n)], True, two)
     g_steps = gather_steps(place, sems, lambda d, lo, num: g_all.at[d], lambda n: g_all.at[pl.ds(0, n)], False, ((0, 0, 1),), True)
+    next(g_steps)
     next(u_steps)
-    next(g_steps)
     finish(ids_steps)
 
     first_e = (me * local).astype(F32)
@@ -323,6 +327,9 @@
 
     lax.fori_loop(0, group, find, 0)
     next(u_steps)
+    for _ in range(3):
+        next(g_steps)
+    next(dy_steps, None)
     next(dy_steps, None)
     m_flat = m_s[...].reshape(group * 8, toks)
     after = (iota((toks, toks), 0) < iota((toks, toks), 1)).astype(F32).astype(BF16)
@@ -330,7 +337,6 @@
     r_s[...] = r_flat.reshape(group, 8, toks)
     next(u_steps)
     next(dy_steps, None)
-    next(g_steps, None)
     slot = iota((cap, toks), 0).astype(F32)
 
     def build(i, _):
@@ -352,9 +358,10 @@
             take_rows(g * per + b, dy_all, rdy_s)
         return 0
 
-    while next(u_steps, place) is None:
+    for _ in range(9):
+        next(u_steps)
         next(dy_steps, None)
-        next(g_steps, None)
+        next(dy_steps, None)
     for copy in experts_in:
         copy.wait()
 
@@ -403,12 +410,19 @@
                 for j in range(2):
                     relay[part, p, j, 0] = u_all[p * side + 2 * p + j, pl.ds(part * both, both), :]
 
-    def take_u(g, _):
-        for b in range(per):
-            take_rows(g * per + b, u_all, ru_s)
-        return 0
-
-    lax.fori_loop(0, groups, take_u, 0)
+    def take_u(dc):
+        def body(g, _):
+            for b in range(2):
+                for d2 in range(side):
+                    take_rows((2 * g + b) * per + dc * side + d2, u_all, ru_s)
+            return 0
+        lax.fori_loop(0, side // 2, body, 0)
+
+    take_u(0)
+    next(u_steps)
+    next(dy_steps, None)
+    take_u(1)
+    finish(u_steps)
 
     def forward(step, _):
         g = lax.rem(step + side // 2, side)
@@ -598,7 +612,7 @@
         sems.copy(at, at, k_rows[part], k_first, me).wait_send()
         sems.copy(sums.at[part], sums.at[part], k_sums[part], k_second, me).wait_send()
     sems.copy(small, small, k_smalls, k_small, me).wait_send()
-    assert (sems.n_send, sems.n_recv) == (N_SEND, N_RECV), (sems.n_send, sems.n_recv)
+    assert (sems.n_send, sems.n_recv) == (N_SEND, N_RECV)
 
 
 def settle_kernel(*refs):

time: 141 us -> 135 us (0.957)
  Pallas kernels: 140 us -> 134 us
    pallas_call x1, Pallas kernels: 138 us -> 132 us  [device_step(): pl.pallas_call(functools.partial(layer_kernel, group, experts, cap), out_...]
where the time goes in v5:
time: 135 us
  Pallas kernels  134 us (99%)
    pallas_call x1, Pallas kernels, device_step(): pl.pallas_call(functools.partial(layer_kernel, group, experts, cap), out_...  132 us

profile of v5, /device:TPU:97, one launch (start us, length us, event | category | flops | bytes accessed | tf_op | source)
XLA Modules:
  0.0 134.9 jit_solution(10423337766611295401)
XLA Ops:
  0.6 131.6 %layer.1 = (bf16[256,512]{1,0:T(8,128)(2,1)}, bf16[256,512]{1,0:T(8,128)(2,1)}, bf16[2,512,256]{2,1,0:T(8,128)(2,1)}, bf16[2,512,256]{2,1,0:T(8,128)(2,1)}, bf16[2,256,512]{2,1,0:T(8,128)(2,1)}) custom-call(bf16[256,512]{1,0:T(8,128)(2,1)} %x_ref.1, s32[8,256]{1,0:T(8,128)} %bitcast.3, bf16[256,512]{1,0:T(8,128)(2,1)} %dy_ref.1, bf16[16,512]{1,0:T(8,128)(2,1)} %wq_ref.1, ...), custom_call_target="tpu_custom_call" | custom-call | tf_op jit(solution)/shard_map/layer/pallas_call | solution.py:666
  132.3 2.4 %settle.1 = (bf16[256,512]{1,0:T(8,128)(2,1)}, bf16[256,512]{1,0:T(8,128)(2,1)}, bf16[2,512,256]{2,1,0:T(8,128)(2,1)}, bf16[2,512,256]{2,1,0:T(8,128)(2,1)}, bf16[2,256,512]{2,1,0:T(8,128)(2,1)}) custom-call(bf16[256,512]{1,0:T(8,128)(2,1)} %get-tuple-element.10.refs_0_, bf16[256,512]{1,0:T(8,128)(2,1)} %get-tuple-element.11.refs_1_, ...), custom_call_target="tpu_custom_call" | custom-call | tf_op jit(solution)/shard_map/settle/pallas_call | solution.py:635

commit v6 on v5

--- a/solution.py
+++ b/solution.py
@@ -203,10 +203,10 @@
     return dy, dx, dc
 
 
-def layer_kernel(group, experts, cap, x_ref, idst_ref, dy_ref, wq_ref, wk_ref, wv_ref, wo_ref, wr_ref, wg_in, wu_in, wd_in,
+def layer_kernel(group, experts, cap, x_in, idst_in, dy_in, wq_ref, wk_ref, wv_ref, wo_ref, wr_in, wg_in, wu_in, wd_in,
                  y_ref, gx_ref, gg_ref, gu_ref, gd_ref,
-                 w_full, u_all, dy_all, ids_all, g_all, m_s, r_s, pick_s, ru_s, rdy_s, ag_s, au_s, mid_s, dag_s, dau_s,
-                 wg_ref, wu_ref, wd_ref, relay, sums, total, small, smalls, prob_s, q_s, k_s, v_s, o_s, hid_s, place_s, gg_s, gu_s, gd_s, y_s,
+                 w_full, u_all, dy_all, ids_all, g_all, m_s, pick_s, ru_s, rdy_s, ag_s, au_s, mid_s, dag_s, dau_s,
+                 x_ref, idst_ref, dy_ref, wr_ref, wg_ref, wu_ref, wd_ref, relay, sums, total, small, smalls, prob_s, q_s, k_s, v_s, o_s, hid_s, place_s, gd_s,
                  lsem, ssem, rsem):
     place = Place(group)
     me = place.me
@@ -224,13 +224,18 @@
     own_w = [pltpu.make_async_copy(w, w_full.at[i, rows_of(me)], lsem.at[i]) for i, w in enumerate((wq_ref, wk_ref, wv_ref, wo_ref))]
     experts_in = [pltpu.make_async_copy(src, dst, lsem.at[4 + i])
                   for i, (src, dst) in enumerate(((wg_in, wg_ref), (wu_in, wu_ref), (wd_in, wd_ref)))]
-    for copy in own_w + experts_in:
-        copy.start()
     sem = pltpu.get_barrier_semaphore()
     peers = near_peers(place)
     for peer in peers:
         pl.semaphore_signal(sem, inc=1, device_id={AXIS: peer}, device_id_type=pl.DeviceIdType.MESH)
 
+    tokens_in = [pltpu.make_async_copy(src, dst, lsem.at[7 + i])
+                 for i, (src, dst) in enumerate(((idst_in, idst_ref), (x_in, x_ref), (dy_in, dy_ref), (wr_in, wr_ref)))]
+    for copy in tokens_in + own_w + experts_in:
+        copy.start()
+
+    for copy in tokens_in:
+        copy.wait()
     dy_all[me] = dy_ref[...]
     idst = idst_ref[...].astype(F32)
     ids_all[me] = idst
@@ -286,7 +291,7 @@
             s = jnp.where(causal, mm(half(qp, hf), kp, NT) * scale, -1e30)
             e = jnp.exp(s - jnp.max(s, axis=-1, keepdims=True))
             p = e / jnp.sum(e, axis=-1, keepdims=True)
-            prob_s[2 * pair + hf] = p
+            prob_s[2 * pair + hf] = jnp.transpose(p)
             outs.append(mm(p.astype(BF16), vp))
         o_s[:, lanes] = jnp.where(low, outs[0], outs[1]).astype(BF16)
         if pair >= 3:
@@ -334,13 +339,13 @@
     m_flat = m_s[...].reshape(group * 8, toks)
     after = (iota((toks, toks), 0) < iota((toks, toks), 1)).astype(F32).astype(BF16)
     r_flat = jnp.where(m_flat > 0.0, mm(m_flat.astype(BF16), after), -1.0)
-    r_s[...] = r_flat.reshape(group, 8, toks)
+    m_s[...] = r_flat.reshape(group, 8, toks)
     next(u_steps)
     next(dy_steps, None)
     slot = iota((cap, toks), 0).astype(F32)
 
     def build(i, _):
-        r = r_s[i]
+        r = m_s[i]
         for e in range(local):
             pick_s[i, pl.ds(e * cap, cap), :] = jnp.where(slot == r[e:e + 1, :], 1.0, 0.0).astype(BF16)
         return 0
@@ -475,13 +480,13 @@
 
     def weights(e, _):
         gd_s[e] = mm(mid_s[e], rdy_s[e], TN).astype(BF16)
-        gg_s[e] = mm(ru_s[e], dag_s[e], TN).astype(BF16)
-        gu_s[e] = mm(ru_s[e], dau_s[e], TN).astype(BF16)
+        mid_s[e, pl.ds(0, d_model), :] = mm(ru_s[e], dag_s[e], TN).astype(BF16)
+        dag_s[e, pl.ds(0, d_model), :] = mm(ru_s[e], dau_s[e], TN).astype(BF16)
         return 0
 
     lax.fori_loop(0, local, weights, 0)
     grads_out = [pltpu.make_async_copy(src, dst, lsem.at[i])
-                 for i, (src, dst) in enumerate(((gg_s, gg_ref), (gu_s, gu_ref), (gd_s, gd_ref), (y_s, y_ref)))]
+                 for i, (src, dst) in enumerate(((mid_s.at[:, pl.ds(0, d_model)], gg_ref), (dag_s.at[:, pl.ds(0, d_model)], gu_ref), (gd_s, gd_ref), (o_s, y_ref)))]
     for copy in grads_out[:3]:
         copy.start()
 
@@ -568,7 +573,7 @@
     sems.copy(total.at[0, rest], total.at[0, rest], k_sums[0], k_second, me).wait_recv()
     sems.copy(smalls.at[rest], smalls.at[rest], k_smalls, k_small, me).wait_recv()
     dyv = dy_ref[...]
-    y_s[...] = (hid_s[...].astype(F32) + ((total[0, 0] + total[0, 1]) + (total[0, 2] + total[0, 3]))).astype(BF16)
+    o_s[...] = (hid_s[...].astype(F32) + ((total[0, 0] + total[0, 1]) + (total[0, 2] + total[0, 3]))).astype(BF16)
     grads_out[3].start()
     m_col = iota((experts, 1), 0)
     owner = jnp.zeros((experts, 1), F32)
@@ -586,6 +591,7 @@
     h = hid_s[...].astype(F32)
     h_inv = inv_rms(h)
     g_hid = (dyv.astype(F32) + rms_back(h, h_inv, gn)).astype(BF16)
+    grads_out[3].wait()
     o_s[...] = mm(g_hid, w_full[3], NT).astype(BF16)
     g_xn = jnp.zeros((toks, d_model), F32)
     for pair in range(pairs):
@@ -593,19 +599,19 @@
         qp, kp, vp, dop = q_s[:, lanes], k_s[:, lanes], v_s[:, lanes], o_s[:, lanes]
         dq, dk, dv = [], [], []
         for hf in range(2):
-            p = prob_s[2 * pair + hf]
-            dp = mm(half(dop, hf), vp, NT)
-            ds = (p * (dp - jnp.sum(dp * p, axis=-1, keepdims=True)) * scale).astype(BF16)
-            dq.append(mm(ds, kp))
-            dk.append(mm(ds, qp, TN))
-            dv.append(mm(p.astype(BF16), dop, TN))
+            p_t = prob_s[2 * pair + hf]
+            dp_t = mm(vp, half(dop, hf), NT)
+            ds_t = (p_t * (dp_t - jnp.sum(dp_t * p_t, axis=0, keepdims=True)) * scale).astype(BF16)
+            dq.append(mm(ds_t, kp, TN))
+            dk.append(mm(ds_t, qp))
+            dv.append(mm(p_t.astype(BF16), dop))
         for i, parts in enumerate((dq, dk, dv)):
             grad = jnp.where(low, parts[0], parts[1]).astype(BF16)
             g_xn += mm(grad, w_full[i, :, lanes], NT)
     x = x_ref[...].astype(F32)
     gx_ref[...] = (g_hid.astype(F32) + rms_back(x, inv_rms(x), g_xn)).astype(BF16)
 
-    for copy in grads_out:
+    for copy in grads_out[:3]:
         copy.wait()
     for part in range(2):
         at = relay.at[part, :, :, pl.ds(1, per - 1)]
@@ -667,21 +673,22 @@
             functools.partial(layer_kernel, group, experts, cap),
             out_shape=[shape(x_tokens.shape, BF16), shape(x_tokens.shape, BF16), shape(w_gate.shape, BF16),
                        shape(w_up.shape, BF16), shape(w_down.shape, BF16)],
-            in_specs=[in_vmem] * 3 + [in_hbm] * 4 + [in_vmem] + [in_hbm] * 3,
+            in_specs=[in_hbm] * 11,
             out_specs=[in_hbm, in_vmem] + [in_hbm] * 3,
             scratch_shapes=[
                 vm((4, group * w_q.shape[0], d_model), BF16), vm((group, toks, d_model), BF16), vm((group, toks, d_model), BF16),
-                vm((group, choices, toks), F32), vm((group, choices, toks), F32), vm((group, 8, toks), F32), vm((group, 8, toks), F32),
+                vm((group, choices, toks), F32), vm((group, choices, toks), F32), vm((group, 8, toks), F32),
                 vm((group, local * cap, toks), BF16), vm((local, rows, d_model), BF16), vm((local, rows, d_model), BF16),
                 vm((local, rows, ff), F32), vm((local, rows, ff), F32),
                 vm((local, rows, ff), BF16), vm((local, rows, ff), BF16), vm((local, rows, ff), BF16),
+                square, vm((choices, toks), jnp.int32), square, vm((experts, d_model), F32),
                 vm(w_gate.shape, BF16), vm(w_up.shape, BF16), vm(w_down.shape, BF16), vm((2, 2, 2, per, local * cap, d_model), BF16),
                 vm((2, side - 1, toks, d_model), F32), vm((2, side, toks, d_model), F32),
                 vm((side - 1, experts // side, toks), F32), vm((side, experts // side, toks), F32),
                 vm((heads, toks, toks), F32), square, square, square, square, square,
                 vm((group // per, toks, per * local * cap), BF16),
-                vm(w_gate.shape, BF16), vm(w_up.shape, BF16), vm(w_down.shape, BF16), square,
-                pltpu.SemaphoreType.DMA((7,)), pltpu.SemaphoreType.DMA((N_SEND,)), pltpu.SemaphoreType.DMA((N_RECV,))],
+                vm(w_down.shape, BF16),
+                pltpu.SemaphoreType.DMA((11,)), pltpu.SemaphoreType.DMA((N_SEND,)), pltpu.SemaphoreType.DMA((N_RECV,))],
             compiler_params=pltpu.CompilerParams(collective_id=1, has_side_effects=True, vmem_limit_bytes=67043328),
             name='layer')(x_tokens, expert_ids.T, grad_y, w_q, w_k, w_v, w_o, w_router.T, w_gate, w_up, w_down)
         return settle(*outs)

time: 135 us -> 134 us (level)
  no operation moved by 1% of the time
where the time goes in v6:
time: 134 us
  Pallas kernels  133 us (99%)
    pallas_call x1, Pallas kernels, device_step(): pl.pallas_call(functools.partial(layer_kernel, group, experts, cap), out_...  130 us

profile of v6, /device:TPU:97, one launch (start us, length us, event | category | flops | bytes accessed | tf_op | source)
XLA Modules:
  0.0 133.7 jit_solution(281930495746025792)
XLA Ops:
  0.6 130.4 %layer.1 = (bf16[256,512]{1,0:T(8,128)(2,1)}, bf16[256,512]{1,0:T(8,128)(2,1)}, bf16[2,512,256]{2,1,0:T(8,128)(2,1)}, bf16[2,512,256]{2,1,0:T(8,128)(2,1)}, bf16[2,256,512]{2,1,0:T(8,128)(2,1)}) custom-call(bf16[256,512]{1,0:T(8,128)(2,1)} %x_in.1, s32[8,256]{1,0:T(8,128)} %bitcast.3, bf16[256,512]{1,0:T(8,128)(2,1)} %dy_in.1, bf16[16,512]{1,0:T(8,128)(2,1)} %wq_ref.1, ...), custom_call_target="tpu_custom_call" | custom-call | tf_op jit(solution)/shard_map/layer/pallas_call | solution.py:672
  131.0 2.4 %settle.1 = (bf16[256,512]{1,0:T(8,128)(2,1)}, bf16[256,512]{1,0:T(8,128)(2,1)}, bf16[2,512,256]{2,1,0:T(8,128)(2,1)}, bf16[2,512,256]{2,1,0:T(8,128)(2,1)}, bf16[2,256,512]{2,1,0:T(8,128)(2,1)}) custom-call(bf16[256,512]{1,0:T(8,128)(2,1)} %get-tuple-element.10.refs_0_, bf16[256,512]{1,0:T(8,128)(2,1)} %get-tuple-element.11.refs_1_, ...), custom_call_target="tpu_custom_call" | custom-call | tf_op jit(solution)/shard_map/settle/pallas_call | solution.py:641

commit v7 on v6

--- a/solution.py
+++ b/solution.py
@@ -609,9 +609,11 @@
             grad = jnp.where(low, parts[0], parts[1]).astype(BF16)
             g_xn += mm(grad, w_full[i, :, lanes], NT)
     x = x_ref[...].astype(F32)
-    gx_ref[...] = (g_hid.astype(F32) + rms_back(x, inv_rms(x), g_xn)).astype(BF16)
-
-    for copy in grads_out[:3]:
+    hid_s[...] = (g_hid.astype(F32) + rms_back(x, inv_rms(x), g_xn)).astype(BF16)
+    gx_out = pltpu.make_async_copy(hid_s, gx_ref, lsem.at[4])
+    gx_out.start()
+
+    for copy in grads_out[:3] + [gx_out]:
         copy.wait()
     for part in range(2):
         at = relay.at[part, :, :, pl.ds(1, per - 1)]
@@ -674,7 +676,7 @@
             out_shape=[shape(x_tokens.shape, BF16), shape(x_tokens.shape, BF16), shape(w_gate.shape, BF16),
                        shape(w_up.shape, BF16), shape(w_down.shape, BF16)],
             in_specs=[in_hbm] * 11,
-            out_specs=[in_hbm, in_vmem] + [in_hbm] * 3,
+            out_specs=[in_hbm] * 5,
             scratch_shapes=[
                 vm((4, group * w_q.shape[0], d_model), BF16), vm((group, toks, d_model), BF16), vm((group, toks, d_model), BF16),
                 vm((group, choices, toks), F32), vm((group, choices, toks), F32), vm((group, 8, toks), F32),

time: 134 us -> 134 us (level)
  no operation moved by 1% of the time
where the time goes in v7:
time: 134 us
  Pallas kernels  133 us (99%)
    pallas_call x1, Pallas kernels, device_step(): pl.pallas_call(functools.partial(layer_kernel, group, experts, cap), out_...  130 us

profile of v7, /device:TPU:97, one launch (start us, length us, event | category | flops | bytes accessed | tf_op | source)
XLA Modules:
  0.0 133.6 jit_solution(9174385071747305277)
XLA Ops:
  0.6 130.4 %layer.1 = (bf16[256,512]{1,0:T(8,128)(2,1)}, bf16[256,512]{1,0:T(8,128)(2,1)}, bf16[2,512,256]{2,1,0:T(8,128)(2,1)}, bf16[2,512,256]{2,1,0:T(8,128)(2,1)}, bf16[2,256,512]{2,1,0:T(8,128)(2,1)}) custom-call(bf16[256,512]{1,0:T(8,128)(2,1)} %x_in.1, s32[8,256]{1,0:T(8,128)} %bitcast.3, bf16[256,512]{1,0:T(8,128)(2,1)} %dy_in.1, bf16[16,512]{1,0:T(8,128)(2,1)} %wq_ref.1, ...), custom_call_target="tpu_custom_call" | custom-call | tf_op jit(solution)/shard_map/layer/pallas_call | solution.py:674
  131.0 2.4 %settle.1 = (bf16[256,512]{1,0:T(8,128)(2,1)}, bf16[256,512]{1,0:T(8,128)(2,1)}, bf16[2,512,256]{2,1,0:T(8,128)(2,1)}, bf16[2,512,256]{2,1,0:T(8,128)(2,1)}, bf16[2,256,512]{2,1,0:T(8,128)(2,1)}) custom-call(bf16[256,512]{1,0:T(8,128)(2,1)} %get-tuple-element.10.refs_0_, bf16[256,512]{1,0:T(8,128)(2,1)} %get-tuple-element.11.refs_1_, ...), custom_call_target="tpu_custom_call" | custom-call | tf_op jit(solution)/shard_map/settle/pallas_call | solution.py:643
